TPU v7x, 128 devices: a whole 4x4x4 slice. The times are simulated.
128 devices in a mesh: row: 8 (over z_lo, x), col: 16 (over z_hi, y, core).
Axes of the slice: x: 4, y: 4, z: 4 (z_hi: 2, z_lo: 2; z = z_hi * 2 + z_lo), core: 2. Of those that a mesh axis runs over, the one named last changes fastest.
Arguments:
- x_iterate: float32 [4096, 4096], P('row', 'col'), may hold values from -6 to 6
- z_inverse: float32 [4096, 4096], P('row', 'col'), may hold values from -0.25 to 0.25
- edge_src: int32 [16, 16, 64], P('row', 'col'), may hold values from 0 to 255
- edge_dst: int32 [16, 16, 64], P('row', 'col'), may hold values from 0 to 255
- edge_count: int32 [16, 16], P('row', 'col'), may hold values from 1 to 64, as said below
Outputs:
- schur_row: float32 [16, 16, 64], P('row', 'col')
Inputs may be any that keep to these rules, and one draw needn't show every extreme that they name: `edge_count`: slots at and beyond a block pair's count are ignored; some block pair has all 64 slots live in every draw.
All inputs are finite; a program needn't handle non-finite values.
Results may differ from a plain program's by a relative error of at most 0.0001.
Values sent between devices are 32-bit elements; how exact they have to be, the bound alone decides.
A program may use at most 64 MiB of HBM per device.

v0:
```python
import jax
import jax.numpy as jnp
from jax import lax
from jax.sharding import PartitionSpec as P

STEPS = 2


def laid_out(parts, dim):
    parts = jnp.moveaxis(parts, 0, dim)
    dims = parts.shape
    return parts.reshape(*dims[:dim], dims[dim] * dims[dim + 1], *dims[dim + 2 :])


def sent_to_all(shard, axis):
    copies = jnp.broadcast_to(shard, (lax.axis_size(axis), *shard.shape))
    return lax.all_to_all(copies, axis, split_axis=0, concat_axis=0, tiled=True)


def gather_directly(shard, axis, dim):
    return laid_out(sent_to_all(shard, axis), dim)


def body(x_iterate, z_inverse, edge_src, edge_dst, edge_count):
    width = x_iterate.shape[1]
    cells = x_iterate.shape[0] // width
    n_col = lax.axis_size("col")
    row_index = lax.axis_index("row")
    col_index = lax.axis_index("col")
    grid_rows = row_index * cells + jnp.arange(cells, dtype=jnp.int32)
    slots = edge_src.shape[2]
    x_cells = x_iterate.reshape(cells, width, width)
    z_cells = z_inverse.reshape(cells, width, width)
    step_range = jnp.arange(STEPS, dtype=jnp.int32)
    src_all = gather_directly(edge_src, "col", 1)
    dest_cols = (col_index - grid_rows[:, None] - step_range[None, :]) % n_col
    send_rows = jnp.take_along_axis(src_all, dest_cols[:, :, None], axis=1)
    x_sent = jnp.take_along_axis(x_cells[:, None, :, :], send_rows[:, :, :, None], axis=2)
    x_got = lax.all_gather(x_sent[:, None], "col", axis=1, tiled=True)
    source_cols = (grid_rows[:, None] + col_index + step_range[None, :]) % n_col
    left = jnp.take_along_axis(x_got, source_cols[:, None, :, None, None], axis=1)[:, 0]
    dst_all = gather_directly(edge_dst, "row", 0)
    dst_flat = dst_all.reshape(dst_all.shape[0], slots)
    dest_rows = (grid_rows[:, None] - col_index - step_range[None, :]) % n_col
    send_cols = jnp.take(dst_flat, dest_rows, axis=0)
    z_sent = jnp.take_along_axis(z_cells[:, None, :, :], send_cols[:, :, None, :], axis=3)
    z_got = gather_directly(z_sent, "row", 0)
    right = jnp.take(z_got, source_cols, axis=0)
    right = jnp.take_along_axis(right, step_range[None, :, None, None, None], axis=2)[:, :, 0]
    values = jnp.einsum("aseb,asbe->ae", left, right, precision=lax.Precision.HIGHEST)
    live = jnp.arange(slots, dtype=jnp.int32)[None, :] < edge_count
    result = jnp.where(live, values, jnp.zeros_like(values))
    return result.reshape(cells, 1, slots)


def solution(mesh):
    return jax.shard_map(
        body,
        mesh=mesh,
        in_specs=(
            P("row", "col"),
            P("row", "col"),
            P("row", "col", None),
            P("row", "col", None),
            P("row", "col"),
        ),
        out_specs=P("row", "col", None),
        check_vma=False,
    )
```

profile of v0, /device:TPU:26, one launch (start us, length us, event | category | flops | bytes accessed | tf_op | source)
XLA Modules:
  0.0 102.3 jit_solution(4375103997723447017)
XLA Ops:
  6.5 0.8 broadcast_bitcast_fusion
  7.3 0.7 reshape.546
  8.0 8.0 %all-to-all-start = ((s32[16,1,128]{2,1,0:T(1,128)}), s32[16,1,128]{2,1,0:T(1,128)S(1)}, u32[]{:S(2)}, u32[]{:S(2)}) async-start(s32[16,1,128]{2,1,0:T(1,128)} %reshape.546), calls=%async_computation | async-start | bytes 16384 | tf_op jit(solution)/shard_map/all_to_all | solution.py:17
  16.2 0.2 fusion.21
  16.5 5.2 %all-to-all-done = s32[16,1,128]{2,1,0:T(1,128)S(1)} async-done(((s32[16,1,128]{2,1,0:T(1,128)}), s32[16,1,128]{2,1,0:T(1,128)S(1)}, u32[]{:S(2)}, u32[]{:S(2)}) %all-to-all-start) | async-done | bytes 8224 | tf_op jit(solution)/shard_map/all_to_all | solution.py:17
  21.6 0.5 broadcast.788
  22.2 0.7 reduce.13
  22.9 0.6 gather_fusion.2
  23.7 2.0 %gather_fusion.3 = f32[256,256]{1,0:T(8,128)S(1)} fusion(f32[2,256,256]{2,1,0:T(8,128)S(1)} %bitcast.48, s32[256]{0:T(256)S(1)} %reshape.502), kind=kCustom, calls=%fused_computation.3 | custom fusion | bytes 526336 | tf_op jit(solution)/shard_map/jit(take_along_axis)/gather | solution.py:38
  25.7 0.8 broadcast_select_fusion.1
  26.6 0.7 reshape.548
  27.3 5.3 %all-to-all-start.1 = ((s32[8,1,128]{2,1,0:T(1,128)}), s32[8,1,128]{2,1,0:T(1,128)S(1)}, u32[]{:S(2)}, u32[]{:S(2)}) async-start(s32[8,1,128]{2,1,0:T(1,128)} %reshape.548), calls=%async_computation.1 | async-start | bytes 8192 | tf_op jit(solution)/shard_map/all_to_all | solution.py:17
  33.2 4.1 %all-to-all-done.1 = s32[8,1,128]{2,1,0:T(1,128)S(1)} async-done(((s32[8,1,128]{2,1,0:T(1,128)}), s32[8,1,128]{2,1,0:T(1,128)S(1)}, u32[]{:S(2)}, u32[]{:S(2)}) %all-to-all-start.1) | async-done | bytes 4128 | tf_op jit(solution)/shard_map/all_to_all | solution.py:17
  37.3 0.7 reduce.12
  38.0 0.6 gather_fusion
  38.8 2.0 %gather_fusion.5 = f32[256,256]{1,0:T(8,128)S(1)} fusion(f32[2,256,256]{1,2,0:T(8,128)S(1)} %copy.12, s32[256]{0:T(256)S(1)} %reshape.516), kind=kCustom, calls=%fused_computation.5 | custom fusion | bytes 526336 | tf_op jit(solution)/shard_map/jit(take_along_axis)/gather | solution.py:46
  41.0 1.6 %broadcast_in_dim.103 = f32[8,2,2,256,64]{3,4,2,1,0:T(8,128)} broadcast(f32[2,2,256,64]{2,3,1,0:T(8,128)S(1)} %select_bitcast_fusion), dimensions={1,2,3,4} | broadcast | bytes 2359296 | tf_op jit(solution)/shard_map/broadcast_in_dim | solution.py:16
  42.5 5.0 %all-to-all-start.2 = ((f32[8,2,2,256,64]{3,4,2,1,0:T(8,128)}), f32[8,2,2,256,64]{3,4,2,1,0:T(8,128)S(1)}, u32[]{:S(2)}, u32[]{:S(2)}) async-start(f32[8,2,2,256,64]{3,4,2,1,0:T(8,128)} %broadcast_in_dim.103), calls=%async_computation.2 | async-start | bytes 4194304 | tf_op jit(solution)/shard_map/all_to_all | solution.py:17
  48.6 23.5 %all-to-all-done.2 = f32[8,2,2,256,64]{3,4,2,1,0:T(8,128)S(1)} async-done(((f32[8,2,2,256,64]{3,4,2,1,0:T(8,128)}), f32[8,2,2,256,64]{3,4,2,1,0:T(8,128)S(1)}, u32[]{:S(2)}, u32[]{:S(2)}) %all-to-all-start.2) | async-done | bytes 2097184 | tf_op jit(solution)/shard_map/all_to_all | solution.py:17
  72.2 0.6 gather_fusion.1
  72.9 0.6 gather_fusion.6
  73.5 18.4 %all-gather.2.cloned.1.call-done = f32[2,16,2,64,256]{4,3,2,0,1:T(8,128)} async-done(((f32[2,1,2,64,256]{4,3,2,0,1:T(8,128)}), f32[2,16,2,64,256]{4,3,2,0,1:T(8,128)}) %all-gather.2.cloned.1.call-update) | async-done | bytes 4194320 | tf_op jit(solution)/shard_map/all_gather | solution.py:39
  91.9 2.8 %gather_fusion.4 = f32[4,64,256]{2,1,0:T(8,128)S(1)} fusion(f32[2,16,2,64,256]{4,3,2,0,1:T(8,128)} %all-gather.2.cloned.1.call-done, s32[4]{0:T(128)S(1)} %reshape.510), kind=kCustom, calls=%fused_computation.4 | custom fusion | bytes 524336 | tf_op jit(solution)/shard_map/jit(take_along_axis)/gather | solution.py:41
  94.8 0.6 compare_select_fusion.25
  (46 shorter events, 3.0 us)
Async XLA Ops:
  6.5 17.2 %copy-start = (f32[512,256]{1,0:T(8,128)S(1)}, f32[512,256]{1,0:T(8,128)}, u32[]{:S(2)}) copy-start(f32[512,256]{1,0:T(8,128)} %param.5) | copy-start | bytes 1572868
  6.5 20.0 %copy-start.2 = (s32[2,1,64]{2,1,0:T(1,128)S(1)}, s32[2,1,64]{2,1,0:T(1,128)}, u32[]{:S(2)}) copy-start(s32[2,1,64]{2,1,0:T(1,128)} %param.8) | copy-start | bytes 1540
  6.5 26.4 %copy-start.1 = (f32[512,256]{1,0:T(8,128)S(1)}, f32[512,256]{1,0:T(8,128)}, u32[]{:S(2)}) copy-start(f32[512,256]{1,0:T(8,128)} %param.6) | copy-start | bytes 1572868
  8.0 13.6 %all-to-all-start = ((s32[16,1,128]{2,1,0:T(1,128)}), s32[16,1,128]{2,1,0:T(1,128)S(1)}, u32[]{:S(2)}, u32[]{:S(2)}) async-start(s32[16,1,128]{2,1,0:T(1,128)} %reshape.546), calls=%async_computation | async-start | bytes 16384 | tf_op jit(solution)/shard_map/all_to_all | solution.py:17
  16.0 75.8 %all-gather.2.cloned.1.call-start = ((), (), s32[]{:S(2)}) async-start(), calls=%async_computation.3 | async-start | bytes 4456448 | tf_op jit(solution)/shard_map/all_gather | solution.py:39
  27.3 10.0 %all-to-all-start.1 = ((s32[8,1,128]{2,1,0:T(1,128)}), s32[8,1,128]{2,1,0:T(1,128)S(1)}, u32[]{:S(2)}, u32[]{:S(2)}) async-start(s32[8,1,128]{2,1,0:T(1,128)} %reshape.548), calls=%async_computation.1 | async-start | bytes 8192 | tf_op jit(solution)/shard_map/all_to_all | solution.py:17
  42.5 29.6 %all-to-all-start.2 = ((f32[8,2,2,256,64]{3,4,2,1,0:T(8,128)}), f32[8,2,2,256,64]{3,4,2,1,0:T(8,128)S(1)}, u32[]{:S(2)}, u32[]{:S(2)}) async-start(f32[8,2,2,256,64]{3,4,2,1,0:T(8,128)} %broadcast_in_dim.103), calls=%async_computation.2 | async-start | bytes 4194304 | tf_op jit(solution)/shard_map/all_to_all | solution.py:17
  72.8 22.0 %copy-start.3 = (s32[2,1]{0,1:T(1,128)S(1)}, s32[2,1]{0,1:T(1,128)}, u32[]{:S(2)}) copy-start(s32[2,1]{0,1:T(1,128)} %param.9) | copy-start | bytes 28
Sparse Core Ops, SparseCore 0:
  26.7 65.1 all-gather.1
where the time goes:
time: 104 us; the launch traced here: 102 us
  waiting for transfers between devices  51.2 us (49%)
  starting transfers between devices  18.3 us (18%)
  local copies, waits for them, and re-layouts  14.2 us (14%)
  between operations  13.6 us (13%)
  other arithmetic  5.05 us (5%)
    all_to_all x3, waiting for transfers between devices, sent_to_all(): return lax.all_to_all(copies, axis, split_axis=0, concat_axis=0, tiled=True)  32.8 us
    all_gather x1, waiting for transfers between devices, body(): x_got = lax.all_gather(x_sent[:, None], 'col', axis=1, tiled=True)  18.4 us
    all_to_all x3, starting transfers between devices, sent_to_all(): return lax.all_to_all(copies, axis, split_axis=0, concat_axis=0, tiled=True)  18.3 us
    gather x2, local copies, waits for them, and re-layouts, body(): jnp.take_along_axis(x_got, source_cols[:, None, :, None, None], axis=1)  2.84 us
    unnamed x17, local copies, waits for them, and re-layouts  2.32 us
    gather x2, local copies, waits for them, and re-layouts, body(): jnp.take_along_axis(x_cells[:, None, :, :], send_rows[:, :, :, None], axi...  2.09 us
    gather x2, local copies, waits for them, and re-layouts, body(): jnp.take_along_axis(z_cells[:, None, :, :], send_cols[:, :, None, :], axi...  2.09 us
  transfers between devices with their start and end apart: 4, of which 4 were waited for; matrix products, arithmetic and copies ran while one was open for 9% of the time, Pallas kernels for 0%

commit v1 on v0

v1 whole, which is shorter than its diff:
```python
import jax
import jax.numpy as jnp
from jax import lax
from jax.experimental import pallas as pl
from jax.experimental.pallas import tpu as pltpu
from jax.sharding import PartitionSpec as P

STEPS = 2
PIECES = 2
MESH = pl.DeviceIdType.MESH


def split_parts(value, parts_ref, index):
    rest = value
    for piece in range(PIECES):
        part = rest.astype(jnp.bfloat16)
        parts_ref[index, piece] = part
        if piece + 1 < PIECES:
            rest = rest - part.astype(jnp.float32)


def picked_rows(indices, parts_ref, index, width):
    count = indices.shape[1]
    down = jnp.transpose(jnp.broadcast_to(indices, (count, count)))
    halves = [
        (down == lax.broadcasted_iota(jnp.int32, (count, count), 1) + first).astype(jnp.float32)
        for first in range(0, width, count)
    ]
    chosen = jnp.concatenate(halves, axis=1).astype(jnp.bfloat16)
    total = jnp.dot(chosen, parts_ref[index, 0], preferred_element_type=jnp.float32)
    for piece in range(1, PIECES):
        total += jnp.dot(chosen, parts_ref[index, piece], preferred_element_type=jnp.float32)
    return total


def kernel(
    x_hbm, z_hbm, src_ref, dst_ref, count_ref, out_ref,
    x_vmem, z_vmem, x_parts, z_parts, index_out, x_index, z_index, x_rows, z_rows,
    local_sem, index_send, x_index_sem, z_index_sem, x_send, z_send, x_recv, z_recv,
):
    row, col = lax.axis_index("row"), lax.axis_index("col")
    n_row, n_col = lax.axis_size("row"), lax.axis_size("col")
    slots = src_ref.shape[2]
    width = x_parts.shape[2]
    cells = 2
    offsets = cells + STEPS - 1

    x_copy = pltpu.make_async_copy(x_hbm, x_vmem, local_sem.at[0])
    z_copy = pltpu.make_async_copy(z_hbm, z_vmem, local_sem.at[1])
    x_copy.start()
    z_copy.start()

    x_owner = [lax.rem(col + cells * row + o, n_col) for o in range(offsets)]
    x_reader = [lax.rem(col - cells * row - o + 2 * n_col, n_col) for o in range(offsets)]
    half = col // cells
    z_owner = [lax.rem(row + half + d, n_row) for d in range(2)]
    z_reader = [lax.rem(row - half - d + 2 * n_row, n_row) for d in range(2)]
    x_self = [x_owner[o] == col for o in range(offsets)]
    z_self = [z_owner[d] == row for d in range(2)]

    barrier = pltpu.get_barrier_semaphore()
    links = [((row, x_owner[o]), (row, x_reader[o]), x_self[o]) for o in range(offsets)]
    links += [((z_owner[d], col), (z_reader[d], col), z_self[d]) for d in range(2)]
    for owner, reader, own in links:
        @pl.when(jnp.logical_not(own))
        def _():
            pl.semaphore_signal(barrier, inc=1, device_id=owner, device_id_type=MESH)
            pl.semaphore_signal(barrier, inc=1, device_id=reader, device_id_type=MESH)

    index_out[0, :, :slots] = src_ref[0]
    index_out[0, :, slots:] = src_ref[1]
    index_out[1, :, :slots] = dst_ref[0]
    index_out[1, :, slots:] = dst_ref[1]

    pl.semaphore_wait(barrier, sum(jnp.where(own, 0, 2) for _, _, own in links))

    def x_index_copy(o):
        return pltpu.make_async_remote_copy(
            src_ref=index_out.at[0], dst_ref=x_index.at[o], send_sem=index_send.at[o], recv_sem=x_index_sem.at[o],
            device_id=(row, x_owner[o]), device_id_type=MESH)

    def z_index_copy(d):
        return pltpu.make_async_remote_copy(
            src_ref=index_out.at[1], dst_ref=z_index.at[d], send_sem=index_send.at[offsets + d], recv_sem=z_index_sem.at[d],
            device_id=(z_owner[d], col), device_id_type=MESH)

    for o in range(offsets):
        @pl.when(jnp.logical_not(x_self[o]))
        def _(o=o):
            x_index_copy(o).start()

        @pl.when(x_self[o])
        def _(o=o):
            x_index[o] = index_out[0]
    for d in range(2):
        @pl.when(jnp.logical_not(z_self[d]))
        def _(d=d):
            z_index_copy(d).start()

        @pl.when(z_self[d])
        def _(d=d):
            z_index[d] = index_out[1]

    x_copy.wait()
    for c in range(cells):
        split_parts(x_vmem[c * width:(c + 1) * width, :], x_parts, c)
    z_copy.wait()
    for b in range(cells):
        split_parts(jnp.transpose(z_vmem[b * width:(b + 1) * width, :]), z_parts, b)

    low = lax.broadcasted_iota(jnp.int32, (1, 2 * slots), 1) < slots
    for o in range(offsets):
        @pl.when(jnp.logical_not(x_self[o]))
        def _(o=o):
            x_index_copy(o).wait_recv()
    first, second, third = (x_index[o] for o in range(offsets))
    turned = pltpu.roll(second, slots, 1)
    x_wanted = [jnp.where(low, first, turned), jnp.where(low, turned, third)]

    def x_copy_out(c, s):
        return pltpu.make_async_remote_copy(
            src_ref=x_rows.at[0, c, s], dst_ref=x_rows.at[1, c, s], send_sem=x_send.at[c, s], recv_sem=x_recv.at[c, s],
            device_id=(row, x_reader[c + s]), device_id_type=MESH)

    for c in range(cells):
        x_rows[0, c] = picked_rows(x_wanted[c], x_parts, c, width).reshape(STEPS, slots, width)
        for s in range(STEPS):
            @pl.when(jnp.logical_not(x_self[c + s]))
            def _(c=c, s=s):
                x_copy_out(c, s).start()

    for d in range(2):
        @pl.when(jnp.logical_not(z_self[d]))
        def _(d=d):
            z_index_copy(d).wait_recv()
    odd = lax.rem(col, 2)
    near, far = z_index[0], z_index[1]
    mixed = jnp.where(low, near, far)
    is_odd = jnp.broadcast_to(odd, (1, 2 * slots)) == 1
    z_wanted = [
        jnp.where(is_odd, pltpu.roll(far, slots, 1), mixed),
        jnp.where(is_odd, mixed, pltpu.roll(near, slots, 1)),
    ]

    def z_target(b, s):
        block = lax.rem(cells * row + b - col - s + 2 * n_col, n_col)
        return block // cells, lax.rem(block, cells)

    def z_copy_out(b, s):
        target, c = z_target(b, s)
        return pltpu.make_async_remote_copy(
            src_ref=z_rows.at[0, b, s], dst_ref=z_rows.at[1, c, s], send_sem=z_send.at[b, s], recv_sem=z_recv.at[c, s],
            device_id=(target, col), device_id_type=MESH)

    for b in range(cells):
        z_rows[0, b] = picked_rows(z_wanted[b], z_parts, b, width).reshape(STEPS, slots, width)
        for s in range(STEPS):
            @pl.when(z_target(b, s)[0] != row)
            def _(b=b, s=s):
                z_copy_out(b, s).start()

    def z_arrival(c, s):
        return pltpu.make_async_remote_copy(
            src_ref=z_rows.at[0, 0, s], dst_ref=z_rows.at[1, c, s], send_sem=z_send.at[0, s], recv_sem=z_recv.at[c, s],
            device_id=(row, col), device_id_type=MESH)

    for c in range(cells):
        total = None
        for s in range(STEPS):
            block = lax.rem(col + cells * row + c + s, n_col)
            z_own = block // cells == row

            @pl.when(jnp.logical_not(x_self[c + s]))
            def _(c=c, s=s):
                x_copy_out(c, s).wait_recv()

            @pl.when(jnp.logical_not(z_own))
            def _(c=c, s=s):
                z_arrival(c, s).wait_recv()

            x_side = jnp.where(x_self[c + s], 0, 1)
            z_side = jnp.where(z_own, 0, 1)
            z_slot = jnp.where(z_own, lax.rem(block, cells), c)
            term = x_rows[x_side, c, s] * z_rows[z_side, z_slot, s]
            total = term if total is None else total + term
        folded = total[:, :slots]
        for at in range(slots, width, slots):
            folded = folded + total[:, at:at + slots]
        values = jnp.sum(jnp.transpose(folded), axis=0, keepdims=True)
        live = lax.broadcasted_iota(jnp.int32, (1, slots), 1) < count_ref[c]
        out_ref[c] = jnp.where(live, values, jnp.zeros_like(values))

    for o in range(offsets):
        @pl.when(jnp.logical_not(x_self[o]))
        def _(o=o):
            x_index_copy(o).wait_send()
    for d in range(2):
        @pl.when(jnp.logical_not(z_self[d]))
        def _(d=d):
            z_index_copy(d).wait_send()
    for c in range(cells):
        for s in range(STEPS):
            @pl.when(jnp.logical_not(x_self[c + s]))
            def _(c=c, s=s):
                x_copy_out(c, s).wait_send()

            @pl.when(z_target(c, s)[0] != row)
            def _(c=c, s=s):
                z_copy_out(c, s).wait_send()


def body(x_iterate, z_inverse, edge_src, edge_dst, edge_count):
    height, width = x_iterate.shape
    cells, _, slots = edge_src.shape
    return pl.pallas_call(
        kernel,
        out_shape=jax.ShapeDtypeStruct((cells, 1, slots), jnp.float32),
        in_specs=[
            pl.BlockSpec(memory_space=pltpu.HBM),
            pl.BlockSpec(memory_space=pltpu.HBM),
            pl.BlockSpec(memory_space=pltpu.VMEM),
            pl.BlockSpec(memory_space=pltpu.VMEM),
            pl.BlockSpec(memory_space=pltpu.SMEM),
        ],
        out_specs=pl.BlockSpec(memory_space=pltpu.VMEM),
        scratch_shapes=[
            pltpu.VMEM((height, width), jnp.float32),
            pltpu.VMEM((height, width), jnp.float32),
            pltpu.VMEM((cells, PIECES, width, width), jnp.bfloat16),
            pltpu.VMEM((cells, PIECES, width, width), jnp.bfloat16),
            pltpu.VMEM((2, 1, cells * slots), jnp.int32),
            pltpu.VMEM((cells + STEPS - 1, 1, cells * slots), jnp.int32),
            pltpu.VMEM((2, 1, cells * slots), jnp.int32),
            pltpu.VMEM((2, cells, STEPS, slots, width), jnp.float32),
            pltpu.VMEM((2, cells, STEPS, slots, width), jnp.float32),
            pltpu.SemaphoreType.DMA((2,)),
            pltpu.SemaphoreType.DMA((cells + STEPS + 1,)),
            pltpu.SemaphoreType.DMA((cells + STEPS - 1,)),
            pltpu.SemaphoreType.DMA((2,)),
            pltpu.SemaphoreType.DMA((cells, STEPS)),
            pltpu.SemaphoreType.DMA((cells, STEPS)),
            pltpu.SemaphoreType.DMA((cells, STEPS)),
            pltpu.SemaphoreType.DMA((cells, STEPS)),
        ],
        compiler_params=pltpu.CompilerParams(collective_id=0, has_side_effects=True),
        name="schur_row",
    )(x_iterate, z_inverse, edge_src, edge_dst, edge_count.reshape(cells))


def solution(mesh):
    return jax.shard_map(
        body,
        mesh=mesh,
        in_specs=(
            P("row", "col"),
            P("row", "col"),
            P("row", "col", None),
            P("row", "col", None),
            P("row", "col"),
        ),
        out_specs=P("row", "col", None),
        check_vma=False,
    )
```

time: 104 us -> 25.1 us (0.24)
  the two profiles are of different devices: /device:TPU:26 before, /device:TPU:42 now
where the time goes in v1:
time: 25.1 us; the launch traced here: 25 us
  Pallas kernels  23.8 us (95%)
  local copies, waits for them, and re-layouts  1.24 us (5%)
    pallas_call x1, Pallas kernels, body(): pl.pallas_call(kernel, out_shape=jax.ShapeDtypeStruct((cells, 1, slots),...  23.8 us
    unnamed x1, local copies, waits for them, and re-layouts  1.24 us

profile of v1, /device:TPU:42, one launch (start us, length us, event | category | flops | bytes accessed | tf_op | source)
XLA Modules:
  0.0 25.0 jit_solution(2193889601433159607)
XLA Ops:
  0.0 23.8 %schur_row.1 = f32[2,1,64]{2,1,0:T(1,128)} custom-call(f32[512,256]{1,0:T(8,128)} %x_hbm.1, f32[512,256]{1,0:T(8,128)} %z_hbm.1, s32[2,1,64]{2,1,0:T(1,128)} %src_ref.1, s32[2,1,64]{2,1,0:T(1,128)} %dst_ref.1, s32[2]{0:T(128)} %bitcast.1), custom_call_target="tpu_custom_call" | custom-call | tf_op jit(solution)/shard_map/schur_row/pallas_call | solution.py:215
  23.8 1.2 %copy.7 = f32[2,1,64]{2,1,0:T(1,128)} copy(f32[2,1,64]{2,1,0:T(1,128)} %schur_row.1) | data formatting | bytes 1024

commit v2 on v1

--- a/solution.py
+++ b/solution.py
@@ -34,21 +34,19 @@
 
 
 def kernel(
-    x_hbm, z_hbm, src_ref, dst_ref, count_ref, out_ref,
-    x_vmem, z_vmem, x_parts, z_parts, index_out, x_index, z_index, x_rows, z_rows,
+    x_hbm, z_hbm, src_hbm, dst_hbm, out_ref,
+    x_vmem, z_vmem, x_parts, z_parts, index_in, index_out, x_index, z_index, x_rows, z_rows,
     local_sem, index_send, x_index_sem, z_index_sem, x_send, z_send, x_recv, z_recv,
 ):
     row, col = lax.axis_index("row"), lax.axis_index("col")
     n_row, n_col = lax.axis_size("row"), lax.axis_size("col")
-    slots = src_ref.shape[2]
+    slots = src_hbm.shape[2]
     width = x_parts.shape[2]
     cells = 2
     offsets = cells + STEPS - 1
 
     x_copy = pltpu.make_async_copy(x_hbm, x_vmem, local_sem.at[0])
     z_copy = pltpu.make_async_copy(z_hbm, z_vmem, local_sem.at[1])
-    x_copy.start()
-    z_copy.start()
 
     x_owner = [lax.rem(col + cells * row + o, n_col) for o in range(offsets)]
     x_reader = [lax.rem(col - cells * row - o + 2 * n_col, n_col) for o in range(offsets)]
@@ -59,20 +57,26 @@
     z_self = [z_owner[d] == row for d in range(2)]
 
     barrier = pltpu.get_barrier_semaphore()
-    links = [((row, x_owner[o]), (row, x_reader[o]), x_self[o]) for o in range(offsets)]
-    links += [((z_owner[d], col), (z_reader[d], col), z_self[d]) for d in range(2)]
-    for owner, reader, own in links:
+    links = [((row, x_reader[o]), x_self[o]) for o in range(offsets)]
+    links += [((z_reader[d], col), z_self[d]) for d in range(2)]
+    for reader, own in links:
         @pl.when(jnp.logical_not(own))
         def _():
-            pl.semaphore_signal(barrier, inc=1, device_id=owner, device_id_type=MESH)
             pl.semaphore_signal(barrier, inc=1, device_id=reader, device_id_type=MESH)
 
-    index_out[0, :, :slots] = src_ref[0]
-    index_out[0, :, slots:] = src_ref[1]
-    index_out[1, :, :slots] = dst_ref[0]
-    index_out[1, :, slots:] = dst_ref[1]
-
-    pl.semaphore_wait(barrier, sum(jnp.where(own, 0, 2) for _, _, own in links))
+    src_copy = pltpu.make_async_copy(src_hbm, index_in.at[0], local_sem.at[2])
+    dst_copy = pltpu.make_async_copy(dst_hbm, index_in.at[1], local_sem.at[3])
+    src_copy.start()
+    dst_copy.start()
+    x_copy.start()
+    z_copy.start()
+    src_copy.wait()
+    dst_copy.wait()
+    for which in range(2):
+        index_out[which, :, :slots] = index_in[which, 0]
+        index_out[which, :, slots:] = index_in[which, 1]
+
+    pl.semaphore_wait(barrier, sum(jnp.where(own, 0, 1) for _, own in links))
 
     def x_index_copy(o):
         return pltpu.make_async_remote_copy(
@@ -187,8 +191,7 @@
         for at in range(slots, width, slots):
             folded = folded + total[:, at:at + slots]
         values = jnp.sum(jnp.transpose(folded), axis=0, keepdims=True)
-        live = lax.broadcasted_iota(jnp.int32, (1, slots), 1) < count_ref[c]
-        out_ref[c] = jnp.where(live, values, jnp.zeros_like(values))
+        out_ref[c] = values
 
     for o in range(offsets):
         @pl.when(jnp.logical_not(x_self[o]))
@@ -212,15 +215,14 @@
 def body(x_iterate, z_inverse, edge_src, edge_dst, edge_count):
     height, width = x_iterate.shape
     cells, _, slots = edge_src.shape
-    return pl.pallas_call(
+    values = pl.pallas_call(
         kernel,
         out_shape=jax.ShapeDtypeStruct((cells, 1, slots), jnp.float32),
         in_specs=[
             pl.BlockSpec(memory_space=pltpu.HBM),
             pl.BlockSpec(memory_space=pltpu.HBM),
-            pl.BlockSpec(memory_space=pltpu.VMEM),
-            pl.BlockSpec(memory_space=pltpu.VMEM),
-            pl.BlockSpec(memory_space=pltpu.SMEM),
+            pl.BlockSpec(memory_space=pltpu.HBM),
+            pl.BlockSpec(memory_space=pltpu.HBM),
         ],
         out_specs=pl.BlockSpec(memory_space=pltpu.VMEM),
         scratch_shapes=[
@@ -228,12 +230,13 @@
             pltpu.VMEM((height, width), jnp.float32),
             pltpu.VMEM((cells, PIECES, width, width), jnp.bfloat16),
             pltpu.VMEM((cells, PIECES, width, width), jnp.bfloat16),
+            pltpu.VMEM((2, cells, 1, slots), jnp.int32),
             pltpu.VMEM((2, 1, cells * slots), jnp.int32),
             pltpu.VMEM((cells + STEPS - 1, 1, cells * slots), jnp.int32),
             pltpu.VMEM((2, 1, cells * slots), jnp.int32),
             pltpu.VMEM((2, cells, STEPS, slots, width), jnp.float32),
             pltpu.VMEM((2, cells, STEPS, slots, width), jnp.float32),
-            pltpu.SemaphoreType.DMA((2,)),
+            pltpu.SemaphoreType.DMA((4,)),
             pltpu.SemaphoreType.DMA((cells + STEPS + 1,)),
             pltpu.SemaphoreType.DMA((cells + STEPS - 1,)),
             pltpu.SemaphoreType.DMA((2,)),
@@ -242,9 +245,11 @@
             pltpu.SemaphoreType.DMA((cells, STEPS)),
             pltpu.SemaphoreType.DMA((cells, STEPS)),
         ],
-        compiler_params=pltpu.CompilerParams(collective_id=0, has_side_effects=True),
+        compiler_params=pltpu.CompilerParams(collective_id=0, has_side_effects=True, vmem_limit_bytes=8 * 2**20),
         name="schur_row",
-    )(x_iterate, z_inverse, edge_src, edge_dst, edge_count.reshape(cells))
+    )(*(pltpu.with_memory_space_constraint(operand, pltpu.HBM) for operand in (x_iterate, z_inverse, edge_src, edge_dst)))
+    live = lax.broadcasted_iota(jnp.int32, values.shape, 2) < edge_count[:, :, None]
+    return jnp.where(live, values, jnp.zeros_like(values))
 
 
 def solution(mesh):

time: 25.1 us -> 23.1 us (0.920)
  Pallas kernels: 23.8 us -> 22.3 us
  local copies, waits for them, and re-layouts: 1.24 us -> 0.01 us
  other arithmetic: 0 us -> 0.63 us
    pallas_call x1, Pallas kernels: 23.8 us -> 22.3 us  [body(): pl.pallas_call(kernel, out_shape=jax.ShapeDtypeStruct((cells, 1, slots),...]
    unnamed x1 -> x2, local copies, waits for them, and re-layouts: 1.24 us -> 0.01 us
    select_n x0 -> x1, other arithmetic: none -> 0.63 us  [body(): return jnp.where(live, values, jnp.zeros_like(values))]
where the time goes in v2:
time: 23.1 us; the launch traced here: 23 us
  Pallas kernels  22.3 us (97%)
  other arithmetic  0.63 us (3%)
    pallas_call x1, Pallas kernels, body(): pl.pallas_call(kernel, out_shape=jax.ShapeDtypeStruct((cells, 1, slots),...  22.3 us
    select_n x1, other arithmetic, body(): return jnp.where(live, values, jnp.zeros_like(values))  0.63 us

profile of v2, /device:TPU:42, one launch (start us, length us, event | category | flops | bytes accessed | tf_op | source)
XLA Modules:
  0.0 23.0 jit_solution(11009954965767042100)
XLA Ops:
  0.0 0.0 copy-start
  0.0 22.3 %schur_row.1 = f32[2,1,64]{2,1,0:T(1,128)S(1)} custom-call(f32[512,256]{1,0:T(8,128)} %x_hbm.1, f32[512,256]{1,0:T(8,128)} %z_hbm.1, s32[2,1,64]{2,1,0:T(1,128)} %src_hbm.1, s32[2,1,64]{2,1,0:T(1,128)} %dst_hbm.1), custom_call_target="tpu_custom_call" | custom-call | tf_op jit(solution)/shard_map/schur_row/pallas_call | solution.py:218
  22.3 0.0 copy-done
  22.3 0.6 %compare_select_fusion = f32[2,1,64]{2,1,0:T(1,128)} fusion(f32[2,1,64]{2,1,0:T(1,128)S(1)} %schur_row.1, s32[2]{0:T(128)S(1)} %bitcast.1), kind=kLoop, calls=%fused_computation | loop fusion | flops 256 | bytes 1032 | tf_op jit(solution)/shard_map/jit(_where)/select_n | solution.py:252
Async XLA Ops:
  0.0 22.3 %copy-start = (s32[2,1]{0,1:T(1,128)S(1)}, s32[2,1]{0,1:T(1,128)}, u32[]{:S(2)}) copy-start(s32[2,1]{0,1:T(1,128)} %param.9) | copy-start | bytes 28

commit v3 on v2

--- a/solution.py
+++ b/solution.py
@@ -35,8 +35,8 @@
 
 def kernel(
     x_hbm, z_hbm, src_hbm, dst_hbm, out_ref,
-    x_vmem, z_vmem, x_parts, z_parts, index_in, index_out, x_index, z_index, x_rows, z_rows,
-    local_sem, index_send, x_index_sem, z_index_sem, x_send, z_send, x_recv, z_recv,
+    x_vmem, z_vmem, x_parts, z_parts, index_in, index_out, x_index, z_index, x_rows, z_rows, given, taken,
+    local_sem, index_send, x_index_sem, z_index_sem, x_send, z_send, x_recv, z_recv, given_sem,
 ):
     row, col = lax.axis_index("row"), lax.axis_index("col")
     n_row, n_col = lax.axis_size("row"), lax.axis_size("col")
@@ -54,11 +54,27 @@
     z_owner = [lax.rem(row + half + d, n_row) for d in range(2)]
     z_reader = [lax.rem(row - half - d + 2 * n_row, n_row) for d in range(2)]
     x_self = [x_owner[o] == col for o in range(offsets)]
+
+    layer, chips = n_row // 2, n_col // 4
+    twin = lax.rem(row + layer, n_row)
+
+    def moved(reader_row, reader_col):
+        diagonal = lax.rem(reader_row, layer) + lax.rem(reader_col, n_col // 2) // 2
+        return jnp.where(diagonal == chips - 1, 0, lax.rem(reader_col // (n_col // 2) + diagonal // chips, 2))
+
+    x_row = [lax.rem(row + layer * moved(row, x_reader[o]), n_row) for o in range(offsets)]
+    x_sends = [jnp.logical_or(x_row[o] != row, jnp.logical_not(x_self[o])) for o in range(offsets)]
+    away = moved(row, col)
+    for_row = lax.rem(row + layer * away, n_row)
+    work_block = [lax.rem(col + cells * for_row + o, n_col) for o in range(offsets)]
+    x_here = [jnp.logical_and(away == 0, work_block[o] == col) for o in range(offsets)]
+    z_here = [work_block[o] // cells == row for o in range(offsets)]
     z_self = [z_owner[d] == row for d in range(2)]
 
     barrier = pltpu.get_barrier_semaphore()
     links = [((row, x_reader[o]), x_self[o]) for o in range(offsets)]
     links += [((z_reader[d], col), z_self[d]) for d in range(2)]
+    pl.semaphore_signal(barrier, inc=1, device_id=(twin, col), device_id_type=MESH)
     for reader, own in links:
         @pl.when(jnp.logical_not(own))
         def _():
@@ -76,7 +92,7 @@
         index_out[which, :, :slots] = index_in[which, 0]
         index_out[which, :, slots:] = index_in[which, 1]
 
-    pl.semaphore_wait(barrier, sum(jnp.where(own, 0, 1) for _, own in links))
+    pl.semaphore_wait(barrier, 1 + sum(jnp.where(own, 0, 1) for _, own in links))
 
     def x_index_copy(o):
         return pltpu.make_async_remote_copy(
@@ -113,26 +129,6 @@
         split_parts(jnp.transpose(z_vmem[b * width:(b + 1) * width, :]), z_parts, b)
 
     low = lax.broadcasted_iota(jnp.int32, (1, 2 * slots), 1) < slots
-    for o in range(offsets):
-        @pl.when(jnp.logical_not(x_self[o]))
-        def _(o=o):
-            x_index_copy(o).wait_recv()
-    first, second, third = (x_index[o] for o in range(offsets))
-    turned = pltpu.roll(second, slots, 1)
-    x_wanted = [jnp.where(low, first, turned), jnp.where(low, turned, third)]
-
-    def x_copy_out(c, s):
-        return pltpu.make_async_remote_copy(
-            src_ref=x_rows.at[0, c, s], dst_ref=x_rows.at[1, c, s], send_sem=x_send.at[c, s], recv_sem=x_recv.at[c, s],
-            device_id=(row, x_reader[c + s]), device_id_type=MESH)
-
-    for c in range(cells):
-        x_rows[0, c] = picked_rows(x_wanted[c], x_parts, c, width).reshape(STEPS, slots, width)
-        for s in range(STEPS):
-            @pl.when(jnp.logical_not(x_self[c + s]))
-            def _(c=c, s=s):
-                x_copy_out(c, s).start()
-
     for d in range(2):
         @pl.when(jnp.logical_not(z_self[d]))
         def _(d=d):
@@ -148,7 +144,8 @@
 
     def z_target(b, s):
         block = lax.rem(cells * row + b - col - s + 2 * n_col, n_col)
-        return block // cells, lax.rem(block, cells)
+        reader = block // cells
+        return lax.rem(reader + layer * moved(reader, col), n_row), lax.rem(block, cells)
 
     def z_copy_out(b, s):
         target, c = z_target(b, s)
@@ -163,6 +160,26 @@
             def _(b=b, s=s):
                 z_copy_out(b, s).start()
 
+    for o in range(offsets):
+        @pl.when(jnp.logical_not(x_self[o]))
+        def _(o=o):
+            x_index_copy(o).wait_recv()
+    first, second, third = (x_index[o] for o in range(offsets))
+    turned = pltpu.roll(second, slots, 1)
+    x_wanted = [jnp.where(low, first, turned), jnp.where(low, turned, third)]
+
+    def x_copy_out(c, s):
+        return pltpu.make_async_remote_copy(
+            src_ref=x_rows.at[0, c, s], dst_ref=x_rows.at[1, c, s], send_sem=x_send.at[c, s], recv_sem=x_recv.at[c, s],
+            device_id=(x_row[c + s], x_reader[c + s]), device_id_type=MESH)
+
+    for c in range(cells):
+        x_rows[0, c] = picked_rows(x_wanted[c], x_parts, c, width).reshape(STEPS, slots, width)
+        for s in range(STEPS):
+            @pl.when(x_sends[c + s])
+            def _(c=c, s=s):
+                x_copy_out(c, s).start()
+
     def z_arrival(c, s):
         return pltpu.make_async_remote_copy(
             src_ref=z_rows.at[0, 0, s], dst_ref=z_rows.at[1, c, s], send_sem=z_send.at[0, s], recv_sem=z_recv.at[c, s],
@@ -171,27 +188,33 @@
     for c in range(cells):
         total = None
         for s in range(STEPS):
-            block = lax.rem(col + cells * row + c + s, n_col)
-            z_own = block // cells == row
-
-            @pl.when(jnp.logical_not(x_self[c + s]))
+            u = c + s
+
+            @pl.when(jnp.logical_not(x_here[u]))
             def _(c=c, s=s):
                 x_copy_out(c, s).wait_recv()
 
-            @pl.when(jnp.logical_not(z_own))
+            @pl.when(jnp.logical_not(z_here[u]))
             def _(c=c, s=s):
                 z_arrival(c, s).wait_recv()
 
-            x_side = jnp.where(x_self[c + s], 0, 1)
-            z_side = jnp.where(z_own, 0, 1)
-            z_slot = jnp.where(z_own, lax.rem(block, cells), c)
+            x_side = jnp.where(x_here[u], 0, 1)
+            z_side = jnp.where(z_here[u], 0, 1)
+            z_slot = jnp.where(z_here[u], lax.rem(work_block[u], cells), c)
             term = x_rows[x_side, c, s] * z_rows[z_side, z_slot, s]
             total = term if total is None else total + term
         folded = total[:, :slots]
         for at in range(slots, width, slots):
             folded = folded + total[:, at:at + slots]
-        values = jnp.sum(jnp.transpose(folded), axis=0, keepdims=True)
-        out_ref[c] = values
+        given[c] = jnp.sum(jnp.transpose(folded), axis=0, keepdims=True)
+
+    given_copy = pltpu.make_async_remote_copy(
+        src_ref=given, dst_ref=taken, send_sem=given_sem.at[0], recv_sem=given_sem.at[1],
+        device_id=(twin, col), device_id_type=MESH)
+
+    @pl.when(away == 1)
+    def _():
+        given_copy.start()
 
     for o in range(offsets):
         @pl.when(jnp.logical_not(x_self[o]))
@@ -203,13 +226,22 @@
             z_index_copy(d).wait_send()
     for c in range(cells):
         for s in range(STEPS):
-            @pl.when(jnp.logical_not(x_self[c + s]))
+            @pl.when(x_sends[c + s])
             def _(c=c, s=s):
                 x_copy_out(c, s).wait_send()
 
             @pl.when(z_target(c, s)[0] != row)
             def _(c=c, s=s):
                 z_copy_out(c, s).wait_send()
+
+    @pl.when(away == 1)
+    def _():
+        given_copy.wait()
+        out_ref[...] = taken[...]
+
+    @pl.when(away == 0)
+    def _():
+        out_ref[...] = given[...]
 
 
 def body(x_iterate, z_inverse, edge_src, edge_dst, edge_count):
@@ -236,6 +268,8 @@
             pltpu.VMEM((2, 1, cells * slots), jnp.int32),
             pltpu.VMEM((2, cells, STEPS, slots, width), jnp.float32),
             pltpu.VMEM((2, cells, STEPS, slots, width), jnp.float32),
+            pltpu.VMEM((cells, 1, slots), jnp.float32),
+            pltpu.VMEM((cells, 1, slots), jnp.float32),
             pltpu.SemaphoreType.DMA((4,)),
             pltpu.SemaphoreType.DMA((cells + STEPS + 1,)),
             pltpu.SemaphoreType.DMA((cells + STEPS - 1,)),
@@ -244,6 +278,7 @@
             pltpu.SemaphoreType.DMA((cells, STEPS)),
             pltpu.SemaphoreType.DMA((cells, STEPS)),
             pltpu.SemaphoreType.DMA((cells, STEPS)),
+            pltpu.SemaphoreType.DMA((2,)),
         ],
         compiler_params=pltpu.CompilerParams(collective_id=0, has_side_effects=True, vmem_limit_bytes=8 * 2**20),
         name="schur_row",

time: 23.1 us -> 22.4 us (0.970)
  the two profiles are of different devices: /device:TPU:42 before, /device:TPU:26 now
where the time goes in v3:
time: 22.4 us; the launch traced here: 22.3 us
  Pallas kernels  21.6 us (96%)
  other arithmetic  0.63 us (3%)
    pallas_call x1, Pallas kernels, body(): pl.pallas_call(kernel, out_shape=jax.ShapeDtypeStruct((cells, 1, slots),...  21.6 us
    select_n x1, other arithmetic, body(): return jnp.where(live, values, jnp.zeros_like(values))  0.63 us

profile of v3, /device:TPU:26, one launch (start us, length us, event | category | flops | bytes accessed | tf_op | source)
XLA Modules:
  0.0 22.3 jit_solution(12528033254852685754)
XLA Ops:
  0.0 0.0 copy-start
  0.0 21.6 %schur_row.1 = f32[2,1,64]{2,1,0:T(1,128)S(1)} custom-call(f32[512,256]{1,0:T(8,128)} %x_hbm.1, f32[512,256]{1,0:T(8,128)} %z_hbm.1, s32[2,1,64]{2,1,0:T(1,128)} %src_hbm.1, s32[2,1,64]{2,1,0:T(1,128)} %dst_hbm.1), custom_call_target="tpu_custom_call" | custom-call | tf_op jit(solution)/shard_map/schur_row/pallas_call | solution.py:250
  21.6 0.0 copy-done
  21.6 0.6 %compare_select_fusion = f32[2,1,64]{2,1,0:T(1,128)} fusion(f32[2,1,64]{2,1,0:T(1,128)S(1)} %schur_row.1, s32[2]{0:T(128)S(1)} %bitcast.1), kind=kLoop, calls=%fused_computation | loop fusion | flops 256 | bytes 1032 | tf_op jit(solution)/shard_map/jit(_where)/select_n | solution.py:287
Async XLA Ops:
  0.0 21.6 %copy-start = (s32[2,1]{0,1:T(1,128)S(1)}, s32[2,1]{0,1:T(1,128)}, u32[]{:S(2)}) copy-start(s32[2,1]{0,1:T(1,128)} %param.9) | copy-start | bytes 28

commit v4 on v0

v4 whole, which is shorter than its diff:
```python
import jax
import jax.numpy as jnp
from jax import lax
from jax.experimental import pallas as pl
from jax.experimental.pallas import tpu as pltpu
from jax.sharding import PartitionSpec as P

STEPS = 2
PIECES = 2
MESH = pl.DeviceIdType.MESH


def split_parts(value, parts_ref, *index):
    rest = value
    for piece in range(PIECES):
        part = rest.astype(jnp.bfloat16)
        parts_ref[(*index, piece)] = part
        if piece + 1 < PIECES:
            rest = rest - part.astype(jnp.float32)


def kernel(
    x_hbm, z_hbm, src_hbm, dst_hbm, out_ref,
    x_vmem, z_vmem, parts, index_in, index_out, wanted, rows_out, rows_in, given, taken,
    local_sem, index_send, index_recv, rows_send, rows_recv, given_sem,
):
    row, col = lax.axis_index("row"), lax.axis_index("col")
    n_row, n_col = lax.axis_size("row"), lax.axis_size("col")
    slots = src_hbm.shape[2]
    width = parts.shape[3]
    cells = 2
    layer, chips = n_row // 2, n_col // 4
    twin = lax.rem(row + layer, n_row)

    def moved(reader_row, reader_col):
        diagonal = lax.rem(reader_row, layer) + lax.rem(reader_col, n_col // 2) // 2
        return jnp.where(diagonal == chips - 1, 0, lax.rem(reader_col // (n_col // 2) + diagonal // chips, 2))

    def working(reader_row, reader_col):
        return lax.rem(reader_row + layer * moved(reader_row, reader_col), n_row)

    x_owner = [lax.rem(col + cells * row + u, n_col) for u in range(3)]
    x_reader = [lax.rem(col - cells * row - u + 2 * n_col, n_col) for u in range(3)]
    half = col // cells
    z_owner = [lax.rem(row + half + d, n_row) for d in range(2)]
    z_reader = [lax.rem(row - half - d + 2 * n_row, n_row) for d in range(2)]
    links = [((row, x_reader[u]), x_owner[u] == col) for u in range(3)]
    links += [((z_reader[d], col), z_owner[d] == row) for d in range(2)]
    barrier = pltpu.get_barrier_semaphore()
    pl.semaphore_signal(barrier, inc=1, device_id=(twin, col), device_id_type=MESH)
    for reader, own in links:
        @pl.when(jnp.logical_not(own))
        def _():
            pl.semaphore_signal(barrier, inc=1, device_id=reader, device_id_type=MESH)

    src_copy = pltpu.make_async_copy(src_hbm, index_in.at[0], local_sem.at[2])
    dst_copy = pltpu.make_async_copy(dst_hbm, index_in.at[1], local_sem.at[3])
    x_copy = pltpu.make_async_copy(x_hbm, x_vmem, local_sem.at[0])
    z_copy = pltpu.make_async_copy(z_hbm, z_vmem, local_sem.at[1])
    src_copy.start()
    dst_copy.start()
    x_copy.start()
    z_copy.start()
    src_copy.wait()
    dst_copy.wait()
    for which in range(2):
        index_out[which, :, :slots] = index_in[which, 0]
        index_out[which, :, slots:] = index_in[which, 1]
    pl.semaphore_wait(barrier, 1 + sum(jnp.where(own, 0, 1) for _, own in links))

    def owner_of(kind, c, s):
        block = lax.rem(col + cells * row + c + s, n_col)
        if kind == 0:
            return row, block, c
        return block // cells, col, lax.rem(block, cells)

    def index_copy(kind, c, s):
        orow, ocol, p = owner_of(kind, c, s)
        return pltpu.make_async_remote_copy(
            src_ref=index_out.at[kind], dst_ref=wanted.at[kind, p, s], send_sem=index_send.at[kind, c, s],
            recv_sem=index_recv.at[kind, p, s], device_id=(orow, ocol), device_id_type=MESH)

    def owner_self(kind, c, s):
        orow, ocol, _ = owner_of(kind, c, s)
        return jnp.logical_and(orow == row, ocol == col)

    tasks = [(k, c, s) for k in (1, 0) for c in range(cells) for s in range(STEPS)]
    for t in tasks:
        @pl.when(jnp.logical_not(owner_self(*t)))
        def _(t=t):
            index_copy(*t).start()

        @pl.when(owner_self(*t))
        def _(t=t):
            wanted[t[0], owner_of(*t)[2], t[2]] = index_out[t[0]]

    x_copy.wait()
    for c in range(cells):
        split_parts(x_vmem[c * width:(c + 1) * width, :], parts, 0, c)
    z_copy.wait()
    for b in range(cells):
        split_parts(jnp.transpose(z_vmem[b * width:(b + 1) * width, :]), parts, 1, b)

    def reader_of(kind, p, s):
        x_col = lax.rem(col - cells * row - p - s + 2 * n_col, n_col)
        block = lax.rem(cells * row + p - col - s + 2 * n_col, n_col)
        isz = kind == 1
        return jnp.where(isz, block // cells, row), jnp.where(isz, col, x_col), jnp.where(isz, lax.rem(block, cells), p)

    def rows_copy(kind, p, s):
        rrow, rcol, c = reader_of(kind, p, s)
        return pltpu.make_async_remote_copy(
            src_ref=rows_out.at[kind, p, s], dst_ref=rows_in.at[kind, c, s], send_sem=rows_send.at[kind, p, s],
            recv_sem=rows_recv.at[kind, c, s], device_id=(working(rrow, rcol), rcol), device_id_type=MESH)

    def stays(kind, p, s):
        rrow, rcol, c = reader_of(kind, p, s)
        return jnp.logical_and(working(rrow, rcol) == row, rcol == col)

    def handle(kind, p, s):
        rrow, rcol, c = reader_of(kind, p, s)

        @pl.when(jnp.logical_not(jnp.logical_and(rrow == row, rcol == col)))
        def _():
            pltpu.make_async_remote_copy(
                src_ref=index_out.at[0], dst_ref=wanted.at[kind, p, s], send_sem=index_send.at[kind, p, s],
                recv_sem=index_recv.at[kind, p, s], device_id=(row, col), device_id_type=MESH).wait_recv()

        both = wanted[kind, p, s]
        upper = jnp.broadcast_to(c, both.shape) == 1
        mine = jnp.where(upper, pltpu.roll(both, slots, 1), both)
        down = jnp.transpose(jnp.broadcast_to(mine, (2 * slots, 2 * slots)))[:slots]
        chosen = jnp.concatenate(
            [(down == lax.broadcasted_iota(jnp.int32, down.shape, 1) + first).astype(jnp.float32)
             for first in range(0, width, 2 * slots)], axis=1).astype(jnp.bfloat16)
        total = jnp.dot(chosen, parts[kind, p, 0], preferred_element_type=jnp.float32)
        for piece in range(1, PIECES):
            total += jnp.dot(chosen, parts[kind, p, piece], preferred_element_type=jnp.float32)
        rows_out[kind, p, s] = total

        @pl.when(jnp.logical_not(stays(kind, p, s)))
        def _():
            rows_copy(kind, p, s).start()

    for t in tasks:
        handle(*t)

    away = moved(row, col)
    for_row = working(row, col)
    for c in range(cells):
        total = None
        for s in range(STEPS):
            block = lax.rem(col + cells * for_row + c + s, n_col)
            x_here = jnp.logical_and(away == 0, block == col)
            z_here = block // cells == row
            for kind, here in ((0, x_here), (1, z_here)):
                @pl.when(jnp.logical_not(here))
                def _(kind=kind, c=c, s=s):
                    pltpu.make_async_remote_copy(
                        src_ref=rows_out.at[kind, c, s], dst_ref=rows_in.at[kind, c, s], send_sem=rows_send.at[kind, c, s],
                        recv_sem=rows_recv.at[kind, c, s], device_id=(row, col), device_id_type=MESH).wait_recv()
            slot = lax.rem(block, cells)
            x_side = jnp.where(x_here, rows_out[0, c, s], rows_in[0, c, s])
            z_side = jnp.where(z_here, rows_out[1, slot, s], rows_in[1, c, s])
            term = x_side * z_side
            total = term if total is None else total + term
        folded = total[:, :slots]
        for at in range(slots, width, slots):
            folded = folded + total[:, at:at + slots]
        given[c] = jnp.sum(jnp.transpose(folded), axis=0, keepdims=True)

    given_copy = pltpu.make_async_remote_copy(
        src_ref=given, dst_ref=taken, send_sem=given_sem.at[0], recv_sem=given_sem.at[1],
        device_id=(twin, col), device_id_type=MESH)

    @pl.when(away == 1)
    def _():
        given_copy.start()

    for t in tasks:
        @pl.when(jnp.logical_not(owner_self(*t)))
        def _(t=t):
            index_copy(*t).wait_send()

        @pl.when(jnp.logical_not(stays(*t)))
        def _(t=t):
            rows_copy(*t).wait_send()

    @pl.when(away == 1)
    def _():
        given_copy.wait()
        out_ref[...] = taken[...]

    @pl.when(away == 0)
    def _():
        out_ref[...] = given[...]


def body(x_iterate, z_inverse, edge_src, edge_dst, edge_count):
    height, width = x_iterate.shape
    cells, _, slots = edge_src.shape
    hbm = pl.BlockSpec(memory_space=pltpu.HBM)
    values = pl.pallas_call(
        kernel,
        out_shape=jax.ShapeDtypeStruct((cells, 1, slots), jnp.float32),
        in_specs=[hbm] * 4,
        out_specs=pl.BlockSpec(memory_space=pltpu.VMEM),
        scratch_shapes=[
            pltpu.VMEM((height, width), jnp.float32),
            pltpu.VMEM((height, width), jnp.float32),
            pltpu.VMEM((2, cells, PIECES, width, width), jnp.bfloat16),
            pltpu.VMEM((2, cells, 1, slots), jnp.int32),
            pltpu.VMEM((2, 1, cells * slots), jnp.int32),
            pltpu.VMEM((2, cells, STEPS, 1, cells * slots), jnp.int32),
            pltpu.VMEM((2, cells, STEPS, slots, width), jnp.float32),
            pltpu.VMEM((2, cells, STEPS, slots, width), jnp.float32),
            pltpu.VMEM((cells, 1, slots), jnp.float32),
            pltpu.VMEM((cells, 1, slots), jnp.float32),
            pltpu.SemaphoreType.DMA((4,)),
            pltpu.SemaphoreType.DMA((2, cells, STEPS)),
            pltpu.SemaphoreType.DMA((2, cells, STEPS)),
            pltpu.SemaphoreType.DMA((2, cells, STEPS)),
            pltpu.SemaphoreType.DMA((2, cells, STEPS)),
            pltpu.SemaphoreType.DMA((2,)),
        ],
        compiler_params=pltpu.CompilerParams(collective_id=0, has_side_effects=True, vmem_limit_bytes=8 * 2**20),
        name="schur_row",
    )(*(pltpu.with_memory_space_constraint(operand, pltpu.HBM) for operand in (x_iterate, z_inverse, edge_src, edge_dst)))
    live = lax.broadcasted_iota(jnp.int32, values.shape, 2) < edge_count[:, :, None]
    return jnp.where(live, values, jnp.zeros_like(values))


def solution(mesh):
    return jax.shard_map(
        body,
        mesh=mesh,
        in_specs=(
            P("row", "col"),
            P("row", "col"),
            P("row", "col", None),
            P("row", "col", None),
            P("row", "col"),
        ),
        out_specs=P("row", "col", None),
        check_vma=False,
    )
```

time: 104 us -> 20.5 us (0.20); the launches traced: 102 us -> 20.4 us
  waiting for transfers between devices: 51.2 us -> 0 us
  Pallas kernels: 0 us -> 19.7 us
  starting transfers between devices: 18.3 us -> 0 us
  local copies, waits for them, and re-layouts: 14.2 us -> 0.01 us
  between operations: 13.6 us -> 0.02 us
  other arithmetic: 5.05 us -> 0.63 us
    all_to_all x3 -> x0, waiting for transfers between devices: 32.8 us -> none  [sent_to_all(): return lax.all_to_all(copies, axis, split_axis=0, concat_axis=0, tiled=True)]
    pallas_call x0 -> x1, Pallas kernels: none -> 19.7 us  [body(): pl.pallas_call(kernel, out_shape=jax.ShapeDtypeStruct((cells, 1, slots),...]
    all_gather x1 -> x0, waiting for transfers between devices: 18.4 us -> none  [body(): x_got = lax.all_gather(x_sent[:, None], 'col', axis=1, tiled=True)]
    all_to_all x3 -> x0, starting transfers between devices: 18.3 us -> none  [sent_to_all(): return lax.all_to_all(copies, axis, split_axis=0, concat_axis=0, tiled=True)]
    gather x11 -> x0, local copies, waits for them, and re-layouts: 9.38 us -> none  [the longest x2 2.84 us: body(): jnp.take_along_axis(x_got, source_cols[:, None, :, None, None], axis=1)]
    unnamed x17 -> x2, local copies, waits for them, and re-layouts: 2.32 us -> 0.01 us
    broadcast_in_dim x1 -> x0, local copies, waits for them, and re-layouts: 1.57 us -> none  [sent_to_all(): copies = jnp.broadcast_to(shard, (lax.axis_size(axis), *shard.shape))]
    select_n x7 -> x1, other arithmetic: 2.18 us -> 0.63 us  [body(): return jnp.where(live, values, jnp.zeros_like(values))]
  transfers between devices with their start and end apart: 4 -> 0, of which waited for: 4 -> 0; matrix products, arithmetic and copies ran while one was open for 9% -> 0% of each run, Pallas kernels for 0% -> 0%
where the time goes in v4:
time: 20.5 us; the launch traced here: 20.4 us
  Pallas kernels  19.7 us (96%)
  other arithmetic  0.63 us (3%)
    pallas_call x1, Pallas kernels, body(): pl.pallas_call(kernel, out_shape=jax.ShapeDtypeStruct((cells, 1, slots),...  19.7 us
    select_n x1, other arithmetic, body(): return jnp.where(live, values, jnp.zeros_like(values))  0.63 us

profile of v4, /device:TPU:26, one launch (start us, length us, event | category | flops | bytes accessed | tf_op | source)
XLA Modules:
  0.0 20.4 jit_solution(4532157014679788680)
XLA Ops:
  0.0 0.0 copy-start
  0.0 19.7 %schur_row.1 = f32[2,1,64]{2,1,0:T(1,128)S(1)} custom-call(f32[512,256]{1,0:T(8,128)} %x_hbm.1, f32[512,256]{1,0:T(8,128)} %z_hbm.1, s32[2,1,64]{2,1,0:T(1,128)} %src_hbm.1, s32[2,1,64]{2,1,0:T(1,128)} %dst_hbm.1), custom_call_target="tpu_custom_call" | custom-call | tf_op jit(solution)/shard_map/schur_row/pallas_call | solution.py:203
  19.7 0.0 copy-done
  19.7 0.6 %compare_select_fusion = f32[2,1,64]{2,1,0:T(1,128)} fusion(f32[2,1,64]{2,1,0:T(1,128)S(1)} %schur_row.1, s32[2]{0:T(128)S(1)} %bitcast.1), kind=kLoop, calls=%fused_computation | loop fusion | flops 256 | bytes 1032 | tf_op jit(solution)/shard_map/jit(_where)/select_n | solution.py:230
Async XLA Ops:
  0.0 19.7 %copy-start = (s32[2,1]{0,1:T(1,128)S(1)}, s32[2,1]{0,1:T(1,128)}, u32[]{:S(2)}) copy-start(s32[2,1]{0,1:T(1,128)} %param.9) | copy-start | bytes 28

commit v5 on v4

--- a/solution.py
+++ b/solution.py
@@ -21,8 +21,8 @@
 
 def kernel(
     x_hbm, z_hbm, src_hbm, dst_hbm, out_ref,
-    x_vmem, z_vmem, parts, index_in, index_out, wanted, rows_out, rows_in, given, taken,
-    local_sem, index_send, index_recv, rows_send, rows_recv, given_sem,
+    x_vmem, z_vmem, parts, index_in, index_out, wanted, rows_out, rows_in, held, near_out, given, taken,
+    local_sem, index_send, index_recv, rows_send, rows_recv, push_sem, near_sem, given_sem,
 ):
     row, col = lax.axis_index("row"), lax.axis_index("col")
     n_row, n_col = lax.axis_size("row"), lax.axis_size("col")
@@ -34,10 +34,26 @@
 
     def moved(reader_row, reader_col):
         diagonal = lax.rem(reader_row, layer) + lax.rem(reader_col, n_col // 2) // 2
-        return jnp.where(diagonal == chips - 1, 0, lax.rem(reader_col // (n_col // 2) + diagonal // chips, 2))
+        return jnp.where(diagonal >= chips - 1, 0, reader_col // (n_col // 2))
 
     def working(reader_row, reader_col):
         return lax.rem(reader_row + layer * moved(reader_row, reader_col), n_row)
+
+    def pushed(reader_row, reader_col, q):
+        x, y = lax.rem(reader_row, layer), lax.rem(reader_col, n_col // 2) // 2
+        early = jnp.logical_and(x + y < chips, reader_col < n_col // 2)
+        return jnp.logical_and(jnp.logical_and(early, (x + 1) // 2 == 1), q == 1)
+
+    core = lax.rem(col, 2)
+    even = col - core
+    for_row = working(row, col)
+    gives_cell = 1 - core
+    gives_to = lax.rem(col - cells * row - gives_cell - 1 + 2 * n_col, n_col)
+    gives = pushed(row, gives_to, gives_cell)
+    holds = pushed(for_row, even, core)
+    giver = (for_row, lax.rem(even + cells * for_row + 1 + core, n_col))
+    near = [pushed(row, even, c) for c in range(cells)]
+    work_near = [pushed(for_row, even, c) for c in range(cells)]
 
     x_owner = [lax.rem(col + cells * row + u, n_col) for u in range(3)]
     x_reader = [lax.rem(col - cells * row - u + 2 * n_col, n_col) for u in range(3)]
@@ -47,7 +63,13 @@
     links = [((row, x_reader[u]), x_owner[u] == col) for u in range(3)]
     links += [((z_reader[d], col), z_owner[d] == row) for d in range(2)]
     barrier = pltpu.get_barrier_semaphore()
-    pl.semaphore_signal(barrier, inc=1, device_id=(twin, col), device_id_type=MESH)
+    for device in ((twin, col), (row, even + 1 - core), (twin, even + 1 - core)):
+        pl.semaphore_signal(barrier, inc=1, device_id=device, device_id_type=MESH)
+
+    @pl.when(holds)
+    def _():
+        pl.semaphore_signal(barrier, inc=1, device_id=giver, device_id_type=MESH)
+
     for reader, own in links:
         @pl.when(jnp.logical_not(own))
         def _():
@@ -66,22 +88,26 @@
     for which in range(2):
         index_out[which, :, :slots] = index_in[which, 0]
         index_out[which, :, slots:] = index_in[which, 1]
-    pl.semaphore_wait(barrier, 1 + sum(jnp.where(own, 0, 1) for _, own in links))
+    pl.semaphore_wait(barrier, 3 + jnp.where(gives, 1, 0) + sum(jnp.where(own, 0, 1) for _, own in links))
+
+    def from_near(c, s):
+        return jnp.logical_and(near[c], core == 1 - s)
 
     def owner_of(kind, c, s):
         block = lax.rem(col + cells * row + c + s, n_col)
         if kind == 0:
-            return row, block, c
-        return block // cells, col, lax.rem(block, cells)
+            close = from_near(c, s)
+            return jnp.where(close, for_row, row), jnp.where(close, even + c, block), jnp.where(close, 0, c), jnp.where(close, 2, 0)
+        return block // cells, col, lax.rem(block, cells), 1
 
     def index_copy(kind, c, s):
-        orow, ocol, p = owner_of(kind, c, s)
+        orow, ocol, p, to = owner_of(kind, c, s)
         return pltpu.make_async_remote_copy(
-            src_ref=index_out.at[kind], dst_ref=wanted.at[kind, p, s], send_sem=index_send.at[kind, c, s],
-            recv_sem=index_recv.at[kind, p, s], device_id=(orow, ocol), device_id_type=MESH)
+            src_ref=index_out.at[kind], dst_ref=wanted.at[to, p, s], send_sem=index_send.at[kind, c, s],
+            recv_sem=index_recv.at[to, p, s], device_id=(orow, ocol), device_id_type=MESH)
 
     def owner_self(kind, c, s):
-        orow, ocol, _ = owner_of(kind, c, s)
+        orow, ocol, _, _ = owner_of(kind, c, s)
         return jnp.logical_and(orow == row, ocol == col)
 
     tasks = [(k, c, s) for k in (1, 0) for c in range(cells) for s in range(STEPS)]
@@ -92,9 +118,18 @@
 
         @pl.when(owner_self(*t))
         def _(t=t):
-            wanted[t[0], owner_of(*t)[2], t[2]] = index_out[t[0]]
+            _, _, p, to = owner_of(*t)
+            wanted[to, p, t[2]] = index_out[t[0]]
 
     x_copy.wait()
+    push_copy = pltpu.make_async_remote_copy(
+        src_ref=x_vmem.at[pl.ds(pl.multiple_of(gives_cell * width, width), width)], dst_ref=held, send_sem=push_sem.at[0],
+        recv_sem=push_sem.at[1], device_id=(working(row, gives_to), gives_to + gives_cell), device_id_type=MESH)
+
+    @pl.when(gives)
+    def _():
+        push_copy.start()
+
     for c in range(cells):
         split_parts(x_vmem[c * width:(c + 1) * width, :], parts, 0, c)
     z_copy.wait()
@@ -126,7 +161,13 @@
                 src_ref=index_out.at[0], dst_ref=wanted.at[kind, p, s], send_sem=index_send.at[kind, p, s],
                 recv_sem=index_recv.at[kind, p, s], device_id=(row, col), device_id_type=MESH).wait_recv()
 
-        both = wanted[kind, p, s]
+        rows_out[kind, p, s] = gathered(wanted[kind, p, s], c, kind, p)
+
+        @pl.when(jnp.logical_not(stays(kind, p, s)))
+        def _():
+            rows_copy(kind, p, s).start()
+
+    def gathered(both, c, kind, p):
         upper = jnp.broadcast_to(c, both.shape) == 1
         mine = jnp.where(upper, pltpu.roll(both, slots, 1), both)
         down = jnp.transpose(jnp.broadcast_to(mine, (2 * slots, 2 * slots)))[:slots]
@@ -136,24 +177,50 @@
         total = jnp.dot(chosen, parts[kind, p, 0], preferred_element_type=jnp.float32)
         for piece in range(1, PIECES):
             total += jnp.dot(chosen, parts[kind, p, piece], preferred_element_type=jnp.float32)
-        rows_out[kind, p, s] = total
-
-        @pl.when(jnp.logical_not(stays(kind, p, s)))
+        return total
+
+    def skips(kind, p):
+        return jnp.logical_and(gives, gives_cell == p) if kind == 0 else row < 0
+
+    for t in tasks:
+        @pl.when(jnp.logical_not(skips(*t[:2])))
+        def _(t=t):
+            handle(*t)
+
+    def near_copy():
+        s = core
+        return pltpu.make_async_remote_copy(
+            src_ref=near_out, dst_ref=rows_in.at[0, core, s], send_sem=near_sem.at[0], recv_sem=rows_recv.at[0, core, s],
+            device_id=(row, even + 1 - core), device_id_type=MESH)
+
+    @pl.when(holds)
+    def _():
+        push_copy.wait_recv()
+        split_parts(held[...], parts, 2, 0)
+        pltpu.make_async_remote_copy(
+            src_ref=index_out.at[0], dst_ref=wanted.at[2, 0, core], send_sem=index_send.at[0, 0, 0],
+            recv_sem=index_recv.at[2, 0, core], device_id=(row, col), device_id_type=MESH).wait_recv()
+        near_out[...] = gathered(wanted[2, 0, core], core, 2, 0)
+        near_copy().start()
+
+        @pl.when(for_row != row)
         def _():
-            rows_copy(kind, p, s).start()
-
-    for t in tasks:
-        handle(*t)
+            pltpu.make_async_remote_copy(
+                src_ref=index_out.at[0], dst_ref=wanted.at[2, 0, 1 - core], send_sem=index_send.at[0, 0, 0],
+                recv_sem=index_recv.at[2, 0, 1 - core], device_id=(row, col), device_id_type=MESH).wait_recv()
+
+        rows_in[0, core, 1 - core] = gathered(wanted[2, 0, 1 - core], core, 2, 0)
 
     away = moved(row, col)
-    for_row = working(row, col)
     for c in range(cells):
         total = None
         for s in range(STEPS):
             block = lax.rem(col + cells * for_row + c + s, n_col)
-            x_here = jnp.logical_and(away == 0, block == col)
+            close = jnp.logical_and(work_near[c], core == 1 - s)
+            x_here = jnp.logical_and(jnp.logical_and(away == 0, block == col), jnp.logical_not(close))
+            x_got = jnp.logical_or(x_here, jnp.logical_and(close, core == c))
             z_here = block // cells == row
-            for kind, here in ((0, x_here), (1, z_here)):
+            for kind, here in ((0, x_got), (1, z_here)):
                 @pl.when(jnp.logical_not(here))
                 def _(kind=kind, c=c, s=s):
                     pltpu.make_async_remote_copy(
@@ -182,9 +249,17 @@
         def _(t=t):
             index_copy(*t).wait_send()
 
-        @pl.when(jnp.logical_not(stays(*t)))
+        @pl.when(jnp.logical_not(jnp.logical_or(stays(*t), skips(*t[:2]))))
         def _(t=t):
             rows_copy(*t).wait_send()
+
+    @pl.when(gives)
+    def _():
+        push_copy.wait_send()
+
+    @pl.when(holds)
+    def _():
+        near_copy().wait_send()
 
     @pl.when(away == 1)
     def _():
@@ -208,22 +283,26 @@
         scratch_shapes=[
             pltpu.VMEM((height, width), jnp.float32),
             pltpu.VMEM((height, width), jnp.float32),
-            pltpu.VMEM((2, cells, PIECES, width, width), jnp.bfloat16),
+            pltpu.VMEM((3, cells, PIECES, width, width), jnp.bfloat16),
             pltpu.VMEM((2, cells, 1, slots), jnp.int32),
             pltpu.VMEM((2, 1, cells * slots), jnp.int32),
-            pltpu.VMEM((2, cells, STEPS, 1, cells * slots), jnp.int32),
+            pltpu.VMEM((3, cells, STEPS, 1, cells * slots), jnp.int32),
             pltpu.VMEM((2, cells, STEPS, slots, width), jnp.float32),
             pltpu.VMEM((2, cells, STEPS, slots, width), jnp.float32),
+            pltpu.VMEM((width, width), jnp.float32),
+            pltpu.VMEM((slots, width), jnp.float32),
             pltpu.VMEM((cells, 1, slots), jnp.float32),
             pltpu.VMEM((cells, 1, slots), jnp.float32),
             pltpu.SemaphoreType.DMA((4,)),
             pltpu.SemaphoreType.DMA((2, cells, STEPS)),
-            pltpu.SemaphoreType.DMA((2, cells, STEPS)),
+            pltpu.SemaphoreType.DMA((3, cells, STEPS)),
             pltpu.SemaphoreType.DMA((2, cells, STEPS)),
             pltpu.SemaphoreType.DMA((2, cells, STEPS)),
             pltpu.SemaphoreType.DMA((2,)),
+            pltpu.SemaphoreType.DMA((1,)),
+            pltpu.SemaphoreType.DMA((2,)),
         ],
-        compiler_params=pltpu.CompilerParams(collective_id=0, has_side_effects=True, vmem_limit_bytes=8 * 2**20),
+        compiler_params=pltpu.CompilerParams(collective_id=0, has_side_effects=True, vmem_limit_bytes=10 * 2**20),
         name="schur_row",
     )(*(pltpu.with_memory_space_constraint(operand, pltpu.HBM) for operand in (x_iterate, z_inverse, edge_src, edge_dst)))
     live = lax.broadcasted_iota(jnp.int32, values.shape, 2) < edge_count[:, :, None]

time: 20.5 us -> 19.5 us (0.951)
  Pallas kernels: 19.7 us -> 18.7 us
    pallas_call x1, Pallas kernels: 19.7 us -> 18.7 us  [body(): pl.pallas_call(kernel, out_shape=jax.ShapeDtypeStruct((cells, 1, slots),...]
where the time goes in v5:
time: 19.5 us; the launch traced here: 19.3 us
  Pallas kernels  18.7 us (96%)
  other arithmetic  0.63 us (3%)
    pallas_call x1, Pallas kernels, body(): pl.pallas_call(kernel, out_shape=jax.ShapeDtypeStruct((cells, 1, slots),...  18.7 us
    select_n x1, other arithmetic, body(): return jnp.where(live, values, jnp.zeros_like(values))  0.63 us

profile of v5, /device:TPU:26, one launch (start us, length us, event | category | flops | bytes accessed | tf_op | source)
XLA Modules:
  0.0 19.3 jit_solution(6767936221664771820)
XLA Ops:
  0.0 0.0 copy-start
  0.0 18.7 %schur_row.1 = f32[2,1,64]{2,1,0:T(1,128)S(1)} custom-call(f32[512,256]{1,0:T(8,128)} %x_hbm.1, f32[512,256]{1,0:T(8,128)} %z_hbm.1, s32[2,1,64]{2,1,0:T(1,128)} %src_hbm.1, s32[2,1,64]{2,1,0:T(1,128)} %dst_hbm.1), custom_call_target="tpu_custom_call" | custom-call | tf_op jit(solution)/shard_map/schur_row/pallas_call | solution.py:278
  18.7 0.0 copy-done
  18.7 0.6 %compare_select_fusion = f32[2,1,64]{2,1,0:T(1,128)} fusion(f32[2,1,64]{2,1,0:T(1,128)S(1)} %schur_row.1, s32[2]{0:T(128)S(1)} %bitcast.1), kind=kLoop, calls=%fused_computation | loop fusion | flops 256 | bytes 1032 | tf_op jit(solution)/shard_map/jit(_where)/select_n | solution.py:309
Async XLA Ops:
  0.0 18.7 %copy-start = (s32[2,1]{0,1:T(1,128)S(1)}, s32[2,1]{0,1:T(1,128)}, u32[]{:S(2)}) copy-start(s32[2,1]{0,1:T(1,128)} %param.9) | copy-start | bytes 28

commit v6 on v5

--- a/solution.py
+++ b/solution.py
@@ -29,6 +29,15 @@
     slots = src_hbm.shape[2]
     width = parts.shape[3]
     cells = 2
+    src_copy = pltpu.make_async_copy(src_hbm, index_in.at[0], local_sem.at[2])
+    dst_copy = pltpu.make_async_copy(dst_hbm, index_in.at[1], local_sem.at[3])
+    x_copy = pltpu.make_async_copy(x_hbm, x_vmem, local_sem.at[0])
+    z_copy = pltpu.make_async_copy(z_hbm, z_vmem, local_sem.at[1])
+    src_copy.start()
+    dst_copy.start()
+    x_copy.start()
+    z_copy.start()
+
     layer, chips = n_row // 2, n_col // 4
     twin = lax.rem(row + layer, n_row)
 
@@ -41,8 +50,8 @@
 
     def pushed(reader_row, reader_col, q):
         x, y = lax.rem(reader_row, layer), lax.rem(reader_col, n_col // 2) // 2
-        early = jnp.logical_and(x + y < chips, reader_col < n_col // 2)
-        return jnp.logical_and(jnp.logical_and(early, (x + 1) // 2 == 1), q == 1)
+        busy = jnp.logical_and((x + 1) // 2 == 1, reader_row != 1)
+        return jnp.logical_and(jnp.logical_and(x + y < chips, jnp.logical_or(reader_col < n_col // 2, busy)), q == 1)
 
     core = lax.rem(col, 2)
     even = col - core
@@ -75,14 +84,6 @@
         def _():
             pl.semaphore_signal(barrier, inc=1, device_id=reader, device_id_type=MESH)
 
-    src_copy = pltpu.make_async_copy(src_hbm, index_in.at[0], local_sem.at[2])
-    dst_copy = pltpu.make_async_copy(dst_hbm, index_in.at[1], local_sem.at[3])
-    x_copy = pltpu.make_async_copy(x_hbm, x_vmem, local_sem.at[0])
-    z_copy = pltpu.make_async_copy(z_hbm, z_vmem, local_sem.at[1])
-    src_copy.start()
-    dst_copy.start()
-    x_copy.start()
-    z_copy.start()
     src_copy.wait()
     dst_copy.wait()
     for which in range(2):
@@ -111,7 +112,7 @@
         return jnp.logical_and(orow == row, ocol == col)
 
     tasks = [(k, c, s) for k in (1, 0) for c in range(cells) for s in range(STEPS)]
-    for t in tasks:
+    for t in tasks[cells * STEPS:] + tasks[:cells * STEPS]:
         @pl.when(jnp.logical_not(owner_self(*t)))
         def _(t=t):
             index_copy(*t).start()
@@ -210,6 +211,16 @@
                 recv_sem=index_recv.at[2, 0, 1 - core], device_id=(row, col), device_id_type=MESH).wait_recv()
 
         rows_in[0, core, 1 - core] = gathered(wanted[2, 0, 1 - core], core, 2, 0)
+
+    for t in tasks:
+        @pl.when(jnp.logical_not(owner_self(*t)))
+        def _(t=t):
+            index_copy(*t).wait_send()
+
+    for t in tasks[:cells * STEPS]:
+        @pl.when(jnp.logical_not(jnp.logical_or(stays(*t), skips(*t[:2]))))
+        def _(t=t):
+            rows_copy(*t).wait_send()
 
     away = moved(row, col)
     for c in range(cells):
@@ -244,11 +255,7 @@
     def _():
         given_copy.start()
 
-    for t in tasks:
-        @pl.when(jnp.logical_not(owner_self(*t)))
-        def _(t=t):
-            index_copy(*t).wait_send()
-
+    for t in tasks[cells * STEPS:]:
         @pl.when(jnp.logical_not(jnp.logical_or(stays(*t), skips(*t[:2]))))
         def _(t=t):
             rows_copy(*t).wait_send()

time: 19.5 us -> 19.4 us (level)
  no operation moved by 1% of the time
where the time goes in v6:
time: 19.4 us; the launch traced here: 19.2 us
  Pallas kernels  18.6 us (96%)
  other arithmetic  0.63 us (3%)
    pallas_call x1, Pallas kernels, body(): pl.pallas_call(kernel, out_shape=jax.ShapeDtypeStruct((cells, 1, slots),...  18.6 us
    select_n x1, other arithmetic, body(): return jnp.where(live, values, jnp.zeros_like(values))  0.63 us

profile of v6, /device:TPU:26, one launch (start us, length us, event | category | flops | bytes accessed | tf_op | source)
XLA Modules:
  0.0 19.2 jit_solution(12358915352184732630)
XLA Ops:
  0.0 0.0 copy-start
  0.0 18.6 %schur_row.1 = f32[2,1,64]{2,1,0:T(1,128)S(1)} custom-call(f32[512,256]{1,0:T(8,128)} %x_hbm.1, f32[512,256]{1,0:T(8,128)} %z_hbm.1, s32[2,1,64]{2,1,0:T(1,128)} %src_hbm.1, s32[2,1,64]{2,1,0:T(1,128)} %dst_hbm.1), custom_call_target="tpu_custom_call" | custom-call | tf_op jit(solution)/shard_map/schur_row/pallas_call | solution.py:285
  18.6 0.0 copy-done
  18.6 0.6 %compare_select_fusion = f32[2,1,64]{2,1,0:T(1,128)} fusion(f32[2,1,64]{2,1,0:T(1,128)S(1)} %schur_row.1, s32[2]{0:T(128)S(1)} %bitcast.1), kind=kLoop, calls=%fused_computation | loop fusion | flops 256 | bytes 1032 | tf_op jit(solution)/shard_map/jit(_where)/select_n | solution.py:316
Async XLA Ops:
  0.0 18.6 %copy-start = (s32[2,1]{0,1:T(1,128)S(1)}, s32[2,1]{0,1:T(1,128)}, u32[]{:S(2)}) copy-start(s32[2,1]{0,1:T(1,128)} %param.9) | copy-start | bytes 28

commit v7 on v6

--- a/solution.py
+++ b/solution.py
@@ -91,37 +91,40 @@
         index_out[which, :, slots:] = index_in[which, 1]
     pl.semaphore_wait(barrier, 3 + jnp.where(gives, 1, 0) + sum(jnp.where(own, 0, 1) for _, own in links))
 
-    def from_near(c, s):
-        return jnp.logical_and(near[c], core == 1 - s)
-
-    def owner_of(kind, c, s):
-        block = lax.rem(col + cells * row + c + s, n_col)
-        if kind == 0:
-            close = from_near(c, s)
-            return jnp.where(close, for_row, row), jnp.where(close, even + c, block), jnp.where(close, 0, c), jnp.where(close, 2, 0)
-        return block // cells, col, lax.rem(block, cells), 1
-
-    def index_copy(kind, c, s):
-        orow, ocol, p, to = owner_of(kind, c, s)
+    messages = [
+        (0, (row, x_owner[u]), u, x_owner[u] == col, jnp.logical_and(near[1], core == 0) if u == 2 else None) for u in range(3)
+    ]
+    messages += [(1, (z_owner[d], col), 3 + d, z_owner[d] == row, None) for d in range(2)]
+    messages += [(0, (for_row, even + 1), 6 - core, jnp.logical_and(for_row == row, core == 1), jnp.logical_not(near[1]))]
+
+    def index_copy(number):
+        which, device, slot, _, _ = messages[number]
         return pltpu.make_async_remote_copy(
-            src_ref=index_out.at[kind], dst_ref=wanted.at[to, p, s], send_sem=index_send.at[kind, c, s],
-            recv_sem=index_recv.at[to, p, s], device_id=(orow, ocol), device_id_type=MESH)
-
-    def owner_self(kind, c, s):
-        orow, ocol, _, _ = owner_of(kind, c, s)
-        return jnp.logical_and(orow == row, ocol == col)
+            src_ref=index_out.at[which], dst_ref=wanted.at[slot], send_sem=index_send.at[number],
+            recv_sem=index_recv.at[slot], device_id=device, device_id_type=MESH)
+
+    def leaves(number):
+        _, _, _, own, dropped = messages[number]
+        out = jnp.logical_not(own)
+        return out if dropped is None else jnp.logical_and(out, jnp.logical_not(dropped))
+
+    for number in (0, 1, 2, 5, 3, 4):
+        @pl.when(leaves(number))
+        def _(number=number):
+            index_copy(number).start()
+
+        which, _, slot, own, dropped = messages[number]
+
+        @pl.when(own if dropped is None else jnp.logical_and(own, jnp.logical_not(dropped)))
+        def _(which=which, slot=slot):
+            wanted[slot] = index_out[which]
+
+    def index_arrival(slot):
+        return pltpu.make_async_remote_copy(
+            src_ref=index_out.at[0], dst_ref=wanted.at[slot], send_sem=index_send.at[0],
+            recv_sem=index_recv.at[slot], device_id=(row, col), device_id_type=MESH)
 
     tasks = [(k, c, s) for k in (1, 0) for c in range(cells) for s in range(STEPS)]
-    for t in tasks[cells * STEPS:] + tasks[:cells * STEPS]:
-        @pl.when(jnp.logical_not(owner_self(*t)))
-        def _(t=t):
-            index_copy(*t).start()
-
-        @pl.when(owner_self(*t))
-        def _(t=t):
-            _, _, p, to = owner_of(*t)
-            wanted[to, p, t[2]] = index_out[t[0]]
-
     x_copy.wait()
     push_copy = pltpu.make_async_remote_copy(
         src_ref=x_vmem.at[pl.ds(pl.multiple_of(gives_cell * width, width), width)], dst_ref=held, send_sem=push_sem.at[0],
@@ -155,14 +158,16 @@
 
     def handle(kind, p, s):
         rrow, rcol, c = reader_of(kind, p, s)
-
-        @pl.when(jnp.logical_not(jnp.logical_and(rrow == row, rcol == col)))
-        def _():
-            pltpu.make_async_remote_copy(
-                src_ref=index_out.at[0], dst_ref=wanted.at[kind, p, s], send_sem=index_send.at[kind, p, s],
-                recv_sem=index_recv.at[kind, p, s], device_id=(row, col), device_id_type=MESH).wait_recv()
-
-        rows_out[kind, p, s] = gathered(wanted[kind, p, s], c, kind, p)
+        slot = p + s if kind == 0 else 3 + (core + c + s) // 2
+        arrives = jnp.logical_not(jnp.logical_and(rrow == row, rcol == col))
+        if kind == 1 and p != s:
+            arrives = jnp.logical_and(arrives, core == p)
+        if (kind, p, s) != (0, 1, 0) and (kind, p, s) != (1, 1, 1):
+            @pl.when(arrives)
+            def _():
+                index_arrival(slot).wait_recv()
+
+        rows_out[kind, p, s] = gathered(wanted[slot], c, kind, p)
 
         @pl.when(jnp.logical_not(stays(kind, p, s)))
         def _():
@@ -198,24 +203,20 @@
     def _():
         push_copy.wait_recv()
         split_parts(held[...], parts, 2, 0)
-        pltpu.make_async_remote_copy(
-            src_ref=index_out.at[0], dst_ref=wanted.at[2, 0, core], send_sem=index_send.at[0, 0, 0],
-            recv_sem=index_recv.at[2, 0, core], device_id=(row, col), device_id_type=MESH).wait_recv()
-        near_out[...] = gathered(wanted[2, 0, core], core, 2, 0)
+        index_arrival(5 + core).wait_recv()
+        near_out[...] = gathered(wanted[5 + core], core, 2, 0)
         near_copy().start()
 
         @pl.when(for_row != row)
         def _():
-            pltpu.make_async_remote_copy(
-                src_ref=index_out.at[0], dst_ref=wanted.at[2, 0, 1 - core], send_sem=index_send.at[0, 0, 0],
-                recv_sem=index_recv.at[2, 0, 1 - core], device_id=(row, col), device_id_type=MESH).wait_recv()
-
-        rows_in[0, core, 1 - core] = gathered(wanted[2, 0, 1 - core], core, 2, 0)
-
-    for t in tasks:
-        @pl.when(jnp.logical_not(owner_self(*t)))
-        def _(t=t):
-            index_copy(*t).wait_send()
+            index_arrival(6 - core).wait_recv()
+
+        rows_in[0, core, 1 - core] = gathered(wanted[6 - core], core, 2, 0)
+
+    for number in range(len(messages)):
+        @pl.when(leaves(number))
+        def _(number=number):
+            index_copy(number).wait_send()
 
     for t in tasks[:cells * STEPS]:
         @pl.when(jnp.logical_not(jnp.logical_or(stays(*t), skips(*t[:2]))))
@@ -293,7 +294,7 @@
             pltpu.VMEM((3, cells, PIECES, width, width), jnp.bfloat16),
             pltpu.VMEM((2, cells, 1, slots), jnp.int32),
             pltpu.VMEM((2, 1, cells * slots), jnp.int32),
-            pltpu.VMEM((3, cells, STEPS, 1, cells * slots), jnp.int32),
+            pltpu.VMEM((7, 1, cells * slots), jnp.int32),
             pltpu.VMEM((2, cells, STEPS, slots, width), jnp.float32),
             pltpu.VMEM((2, cells, STEPS, slots, width), jnp.float32),
             pltpu.VMEM((width, width), jnp.float32),
@@ -301,8 +302,8 @@
             pltpu.VMEM((cells, 1, slots), jnp.float32),
             pltpu.VMEM((cells, 1, slots), jnp.float32),
             pltpu.SemaphoreType.DMA((4,)),
-            pltpu.SemaphoreType.DMA((2, cells, STEPS)),
-            pltpu.SemaphoreType.DMA((3, cells, STEPS)),
+            pltpu.SemaphoreType.DMA((6,)),
+            pltpu.SemaphoreType.DMA((7,)),
             pltpu.SemaphoreType.DMA((2, cells, STEPS)),
             pltpu.SemaphoreType.DMA((2, cells, STEPS)),
             pltpu.SemaphoreType.DMA((2,)),

time: 19.4 us -> 19.3 us (level)
  no operation moved by 1% of the time
where the time goes in v7:
time: 19.3 us; the launch traced here: 19.2 us
  Pallas kernels  18.5 us (96%)
  other arithmetic  0.63 us (3%)
    pallas_call x1, Pallas kernels, body(): pl.pallas_call(kernel, out_shape=jax.ShapeDtypeStruct((cells, 1, slots),...  18.5 us
    select_n x1, other arithmetic, body(): return jnp.where(live, values, jnp.zeros_like(values))  0.63 us

profile of v7, /device:TPU:26, one launch (start us, length us, event | category | flops | bytes accessed | tf_op | source)
XLA Modules:
  0.0 19.2 jit_solution(5075329481717390952)
XLA Ops:
  0.0 0.0 copy-start
  0.0 18.5 %schur_row.1 = f32[2,1,64]{2,1,0:T(1,128)S(1)} custom-call(f32[512,256]{1,0:T(8,128)} %x_hbm.1, f32[512,256]{1,0:T(8,128)} %z_hbm.1, s32[2,1,64]{2,1,0:T(1,128)} %src_hbm.1, s32[2,1,64]{2,1,0:T(1,128)} %dst_hbm.1), custom_call_target="tpu_custom_call" | custom-call | tf_op jit(solution)/shard_map/schur_row/pallas_call | solution.py:286
  18.5 0.0 copy-done
  18.5 0.6 %compare_select_fusion = f32[2,1,64]{2,1,0:T(1,128)} fusion(f32[2,1,64]{2,1,0:T(1,128)S(1)} %schur_row.1, s32[2]{0:T(128)S(1)} %bitcast.1), kind=kLoop, calls=%fused_computation | loop fusion | flops 256 | bytes 1032 | tf_op jit(solution)/shard_map/jit(_where)/select_n | solution.py:317
Async XLA Ops:
  0.0 18.5 %copy-start = (s32[2,1]{0,1:T(1,128)S(1)}, s32[2,1]{0,1:T(1,128)}, u32[]{:S(2)}) copy-start(s32[2,1]{0,1:T(1,128)} %param.9) | copy-start | bytes 28

commit v8 on v7

--- a/solution.py
+++ b/solution.py
@@ -51,7 +51,7 @@
     def pushed(reader_row, reader_col, q):
         x, y = lax.rem(reader_row, layer), lax.rem(reader_col, n_col // 2) // 2
         busy = jnp.logical_and((x + 1) // 2 == 1, reader_row != 1)
-        return jnp.logical_and(jnp.logical_and(x + y < chips, jnp.logical_or(reader_col < n_col // 2, busy)), q == 1)
+        return jnp.logical_and(jnp.logical_or(jnp.logical_and(x + y < chips, jnp.logical_or(reader_col < n_col // 2, busy)), jnp.logical_and(x + y < chips - 1, x == 0)), q == 1)
 
     core = lax.rem(col, 2)
     even = col - core

time: 19.3 us -> 19.3 us (level)
  no operation moved by 1% of the time
where the time goes in v8:
time: 19.3 us; the launch traced here: 19.2 us
  Pallas kernels  18.5 us (96%)
  other arithmetic  0.63 us (3%)
    pallas_call x1, Pallas kernels, body(): pl.pallas_call(kernel, out_shape=jax.ShapeDtypeStruct((cells, 1, slots),...  18.5 us
    select_n x1, other arithmetic, body(): return jnp.where(live, values, jnp.zeros_like(values))  0.63 us

profile of v8, /device:TPU:26, one launch (start us, length us, event | category | flops | bytes accessed | tf_op | source)
XLA Modules:
  0.0 19.2 jit_solution(15597832486383506300)
XLA Ops:
  0.0 0.0 copy-start
  0.0 18.5 %schur_row.1 = f32[2,1,64]{2,1,0:T(1,128)S(1)} custom-call(f32[512,256]{1,0:T(8,128)} %x_hbm.1, f32[512,256]{1,0:T(8,128)} %z_hbm.1, s32[2,1,64]{2,1,0:T(1,128)} %src_hbm.1, s32[2,1,64]{2,1,0:T(1,128)} %dst_hbm.1), custom_call_target="tpu_custom_call" | custom-call | tf_op jit(solution)/shard_map/schur_row/pallas_call | solution.py:286
  18.5 0.0 copy-done
  18.5 0.6 %compare_select_fusion = f32[2,1,64]{2,1,0:T(1,128)} fusion(f32[2,1,64]{2,1,0:T(1,128)S(1)} %schur_row.1, s32[2]{0:T(128)S(1)} %bitcast.1), kind=kLoop, calls=%fused_computation | loop fusion | flops 256 | bytes 1032 | tf_op jit(solution)/shard_map/jit(_where)/select_n | solution.py:317
Async XLA Ops:
  0.0 18.5 %copy-start = (s32[2,1]{0,1:T(1,128)S(1)}, s32[2,1]{0,1:T(1,128)}, u32[]{:S(2)}) copy-start(s32[2,1]{0,1:T(1,128)} %param.9) | copy-start | bytes 28

commit v9 on v8

--- a/solution.py
+++ b/solution.py
@@ -51,7 +51,7 @@
     def pushed(reader_row, reader_col, q):
         x, y = lax.rem(reader_row, layer), lax.rem(reader_col, n_col // 2) // 2
         busy = jnp.logical_and((x + 1) // 2 == 1, reader_row != 1)
-        return jnp.logical_and(jnp.logical_or(jnp.logical_and(x + y < chips, jnp.logical_or(reader_col < n_col // 2, busy)), jnp.logical_and(x + y < chips - 1, x == 0)), q == 1)
+        return jnp.logical_and(jnp.logical_or(jnp.logical_and(x + y < chips, jnp.logical_or(reader_col < n_col // 2, busy)), jnp.logical_and(x + y < chips, lax.rem(x, 3) == 0)), q == 1)
 
     core = lax.rem(col, 2)
     even = col - core

time: 19.3 us -> 19.3 us (level)
  no operation moved by 1% of the time
where the time goes in v9:
time: 19.3 us; the launch traced here: 19.2 us
  Pallas kernels  18.5 us (96%)
  other arithmetic  0.63 us (3%)
    pallas_call x1, Pallas kernels, body(): pl.pallas_call(kernel, out_shape=jax.ShapeDtypeStruct((cells, 1, slots),...  18.5 us
    select_n x1, other arithmetic, body(): return jnp.where(live, values, jnp.zeros_like(values))  0.63 us

profile of v9, /device:TPU:26, one launch (start us, length us, event | category | flops | bytes accessed | tf_op | source)
XLA Modules:
  0.0 19.2 jit_solution(6701547209803672748)
XLA Ops:
  0.0 0.0 copy-start
  0.0 18.5 %schur_row.1 = f32[2,1,64]{2,1,0:T(1,128)S(1)} custom-call(f32[512,256]{1,0:T(8,128)} %x_hbm.1, f32[512,256]{1,0:T(8,128)} %z_hbm.1, s32[2,1,64]{2,1,0:T(1,128)} %src_hbm.1, s32[2,1,64]{2,1,0:T(1,128)} %dst_hbm.1), custom_call_target="tpu_custom_call" | custom-call | tf_op jit(solution)/shard_map/schur_row/pallas_call | solution.py:286
  18.5 0.0 copy-done
  18.5 0.6 %compare_select_fusion = f32[2,1,64]{2,1,0:T(1,128)} fusion(f32[2,1,64]{2,1,0:T(1,128)S(1)} %schur_row.1, s32[2]{0:T(128)S(1)} %bitcast.1), kind=kLoop, calls=%fused_computation | loop fusion | flops 256 | bytes 1032 | tf_op jit(solution)/shard_map/jit(_where)/select_n | solution.py:317
Async XLA Ops:
  0.0 18.5 %copy-start = (s32[2,1]{0,1:T(1,128)S(1)}, s32[2,1]{0,1:T(1,128)}, u32[]{:S(2)}) copy-start(s32[2,1]{0,1:T(1,128)} %param.9) | copy-start | bytes 28

commit v10 on v8

--- a/solution.py
+++ b/solution.py
@@ -43,7 +43,7 @@
 
     def moved(reader_row, reader_col):
         diagonal = lax.rem(reader_row, layer) + lax.rem(reader_col, n_col // 2) // 2
-        return jnp.where(diagonal >= chips - 1, 0, reader_col // (n_col // 2))
+        return jnp.where(diagonal >= 6, 1 - reader_col // (n_col // 2), jnp.where(diagonal >= chips - 1, 0, reader_col // (n_col // 2)))
 
     def working(reader_row, reader_col):
         return lax.rem(reader_row + layer * moved(reader_row, reader_col), n_row)

time: 19.3 us -> 19.3 us (level)
  no operation moved by 1% of the time
where the time goes in v10:
time: 19.3 us; the launch traced here: 19.2 us
  Pallas kernels  18.5 us (96%)
  other arithmetic  0.63 us (3%)
    pallas_call x1, Pallas kernels, body(): pl.pallas_call(kernel, out_shape=jax.ShapeDtypeStruct((cells, 1, slots),...  18.5 us
    select_n x1, other arithmetic, body(): return jnp.where(live, values, jnp.zeros_like(values))  0.63 us

profile of v10, /device:TPU:26, one launch (start us, length us, event | category | flops | bytes accessed | tf_op | source)
XLA Modules:
  0.0 19.2 jit_solution(15145997150944695835)
XLA Ops:
  0.0 0.0 copy-start
  0.0 18.5 %schur_row.1 = f32[2,1,64]{2,1,0:T(1,128)S(1)} custom-call(f32[512,256]{1,0:T(8,128)} %x_hbm.1, f32[512,256]{1,0:T(8,128)} %z_hbm.1, s32[2,1,64]{2,1,0:T(1,128)} %src_hbm.1, s32[2,1,64]{2,1,0:T(1,128)} %dst_hbm.1), custom_call_target="tpu_custom_call" | custom-call | tf_op jit(solution)/shard_map/schur_row/pallas_call | solution.py:286
  18.5 0.0 copy-done
  18.5 0.6 %compare_select_fusion = f32[2,1,64]{2,1,0:T(1,128)} fusion(f32[2,1,64]{2,1,0:T(1,128)S(1)} %schur_row.1, s32[2]{0:T(128)S(1)} %bitcast.1), kind=kLoop, calls=%fused_computation | loop fusion | flops 256 | bytes 1032 | tf_op jit(solution)/shard_map/jit(_where)/select_n | solution.py:317
Async XLA Ops:
  0.0 18.5 %copy-start = (s32[2,1]{0,1:T(1,128)S(1)}, s32[2,1]{0,1:T(1,128)}, u32[]{:S(2)}) copy-start(s32[2,1]{0,1:T(1,128)} %param.9) | copy-start | bytes 28
